TPU v7x, 8 devices: a whole 2x2x1 slice. The times are simulated.
8 devices in a mesh: tp: 2 (over z, y), dp: 4 (over x, core).
Axes of the slice: x: 2, y: 2, z: 1, core: 2. Of those that a mesh axis runs over, the one named last changes fastest.
Arguments:
- h_teacher: bfloat16 [16384, 3584], P('dp')
- h_student: bfloat16 [16384, 1536], P('dp')
- w_teacher: bfloat16 [3584, 4096], P(None, 'tp')
- w_student: bfloat16 [1536, 4096], P(None, 'tp')
Outputs:
- output 1: float32 [], replicated
- output 2: float32 [16384, 1536], P('dp')
- output 3: float32 [1536, 4096], P(None, 'tp')
All inputs are finite; a program needn't handle non-finite values.
Results may differ from a plain program's by a relative error of at most 0.001.
Values sent between devices are 32-bit elements.
A program may use at most 1 GiB of HBM per device.

v0:
```python
import jax
import jax.numpy as jnp
from jax import lax
from jax.sharding import PartitionSpec as P


def solution(mesh):
    dp_size = mesh.shape["dp"]

    def local_step(h_teacher, h_student, w_teacher, w_student):
        tok_total = h_teacher.shape[0] * dp_size
        z_teacher = jnp.dot(h_teacher, w_teacher, preferred_element_type=jnp.float32)
        z_student = jnp.dot(h_student, w_student, preferred_element_type=jnp.float32)
        local_max = jnp.stack([jnp.max(z_teacher, axis=1), jnp.max(z_student, axis=1)], axis=1)
        row_max = lax.pmax(local_max, "tp")
        shift_t = z_teacher - row_max[:, 0:1]
        shift_s = z_student - row_max[:, 1:2]
        exp_t = jnp.exp(shift_t)
        exp_s = jnp.exp(shift_s)
        local_sum = jnp.stack([jnp.sum(exp_t, axis=1), jnp.sum(exp_s, axis=1)], axis=1)
        row_sum = lax.psum(local_sum, "tp")
        log_sum = jnp.log(row_sum)
        prob_t = exp_t / row_sum[:, 0:1]
        prob_s = exp_s / row_sum[:, 1:2]
        kl_part = jnp.sum(prob_t * ((shift_t - log_sum[:, 0:1]) - (shift_s - log_sum[:, 1:2])))
        kl_loss = lax.psum(kl_part, ("tp", "dp")) / tok_total
        dz_student = ((prob_s - prob_t) / tok_total).astype(jnp.bfloat16)
        dh_part = lax.dot_general(dz_student, w_student, (((1,), (1,)), ((), ())),
                                  preferred_element_type=jnp.float32)
        dh_student = lax.psum(dh_part, "tp")
        dw_part = lax.dot_general(h_student, dz_student, (((0,), (0,)), ((), ())),
                                  preferred_element_type=jnp.float32)
        dw_student = lax.psum(dw_part, "dp")
        return kl_loss, dh_student, dw_student

    return jax.shard_map(
        local_step, mesh=mesh,
        in_specs=(P("dp", None), P("dp", None), P(None, "tp"), P(None, "tp")),
        out_specs=(P(), P("dp", None), P(None, "tp")),
        check_vma=False)
```

profile of v0, /device:TPU:0, one launch (start us, length us, event | category | flops | bytes accessed | tf_op | source)
XLA Modules:
  0.0 1049.2 jit_solution(7306903738624855625)
XLA Ops:
  7.2 0.0 all-reduce.5.cloned.1.call-start
  7.2 101.0 %fusion.4 = (f32[4096]{0:T(1024)S(1)}, f32[4096,2048]{0,1:T(8,128)}) fusion(bf16[4096,3584]{1,0:T(8,128)(2,1)} %param.4, bf16[3584,2048]{1,0:T(8,128)(2,1)} %param.6), kind=kOutput, calls=%fused_computation.12 | convolution fusion | flops 60137926656 | bytes 77611008 | tf_op jit(solution)/shard_map/dot_general | solution.py:12
  108.2 34.0 %fusion.3 = (f32[4096]{0:T(1024)S(1)}, f32[4096,2048]{0,1:T(8,128)}) fusion(bf16[4096,1536]{1,0:T(8,128)(2,1)} %param.5, bf16[1536,2048]{1,0:T(8,128)(2,1)} %param.7), kind=kOutput, calls=%fused_computation.11 | convolution fusion | flops 25778188288 | bytes 52445184 | tf_op jit(solution)/shard_map/dot_general | solution.py:13
  142.3 10.3 pmax.7
  152.6 0.0 copy-start
  152.7 13.6 %exponential_reduce_fusion = f32[4096]{0:T(1024)S(1)} fusion(f32[4096,2048]{0,1:T(8,128)} %get-tuple-element.18, f32[4096]{0:T(1024)S(1)} %bitcast.22), kind=kLoop, calls=%fused_computation.2 | loop fusion | flops 16773120 | bytes 33587200 | tf_op jit(solution)/shard_map/reduce_sum | solution.py:20
  166.3 6.6 copy-done
  172.9 5.0 exponential_reduce_fusion.1
  178.0 6.9 psum.28
  185.0 31.6 %multiply_convert_fusion = (bf16[4096,2048]{0,1:T(8,128)(2,1)}, f32[]{:T(128)}) fusion(f32[4096,2048]{0,1:T(8,128)} %get-tuple-element.18, f32[4096,2048]{0,1:T(8,128)} %get-tuple-element.20, f32[4096]{0:T(1024)S(1)} %bitcast.26, f32[4096]{0:T(1024)S(1)} %bitcast.27, f32[4096]{0:T(1024)S(1)} %bitcast.23, f32[4096]{0:T(1024)S(1)} %bitcast.21, ...), kind=kLoop, calls=%fused_computation | loop fusion | flops 100663296 | bytes 83984384 | tf_op jit(solution)/shard_map/convert_element_type | solution.py:27
  216.6 34.1 %convolution_bitcast_fusion = f32[1536,2048]{0,1:T(8,128)} fusion(bf16[4096,2048]{0,1:T(8,128)(2,1)} %get-tuple-element.9, bf16[4096,1536]{1,0:T(8,128)(2,1)} %param.5), kind=kOutput, calls=%fused_computation.5 | convolution fusion | flops 25769803776 | bytes 41943040 | tf_op jit(solution)/shard_map/dot_general | solution.py:31
  250.7 0.0 all-reduce.5.cloned.1.call-update
  250.7 0.0 all-reduce.3.cloned.1.call-start
  250.8 33.9 %fusion.5 = f32[4096,1536]{1,0:T(8,128)} fusion(bf16[4096,2048]{0,1:T(8,128)(2,1)} %get-tuple-element.9, bf16[1536,2048]{1,0:T(8,128)(2,1)} %param.7), kind=kOutput, calls=%fused_computation.13 | convolution fusion | flops 25769803776 | bytes 48234496 | tf_op jit(solution)/shard_map/dot_general | solution.py:28
  284.7 0.0 all-reduce.3.cloned.1.call-update
  284.7 24.4 %psum.29 = f32[]{:T(128)} all-reduce(f32[]{:T(128)} %get-tuple-element.10), channel_id=1, replica_groups=mesh['tp'=2,'dp'=4] {'tp','dp'}, use_global_device_ids=true, to_apply=%region_7.0 | all-reduce | flops 1 | bytes 8 | tf_op jit(solution)/shard_map/psum | solution.py:26
  309.8 158.7 %all-reduce.5.cloned.1.call-done = f32[1536,2048]{0,1:T(8,128)} async-done(((f32[1536,2048]{0,1:T(8,128)}), f32[1536,2048]{0,1:T(8,128)}) %all-reduce.5.cloned.1.call-update) | async-done | bytes 12582928 | tf_op jit(solution)/shard_map/psum | solution.py:33
  468.5 12.6 %copy.8 = f32[1536,2048]{1,0:T(8,128)} copy(f32[1536,2048]{0,1:T(8,128)} %all-reduce.5.cloned.1.call-done) | data formatting | bytes 25165824
  481.1 542.7 %all-reduce.3.cloned.1.call-done = f32[4096,1536]{1,0:T(8,128)} async-done(((f32[4096,1536]{1,0:T(8,128)}), f32[4096,1536]{1,0:T(8,128)}) %all-reduce.3.cloned.1.call-update) | async-done | bytes 25165840 | tf_op jit(solution)/shard_map/psum | solution.py:30
  1023.8 17.5 %copy.11 = f32[4096,1536]{1,0:T(8,128)} copy(f32[4096,1536]{1,0:T(8,128)} %all-reduce.3.cloned.1.call-done) | data formatting | bytes 50331648
  (6 shorter events, 0.2 us)
Async XLA Ops:
  7.2 461.3 %all-reduce.5.cloned.1.call-start = ((), (), s32[]{:S(2)}) async-start(), calls=%async_computation.1 | async-start | bytes 25165824 | tf_op jit(solution)/shard_map/psum | solution.py:33
  152.6 20.3 %copy-start = (f32[4096,2048]{0,1:T(8,128)S(1)}, f32[4096,2048]{0,1:T(8,128)}, u32[]{:S(2)}) copy-start(f32[4096,2048]{0,1:T(8,128)} %get-tuple-element.20) | copy-start | bytes 100663296
  250.7 773.1 %all-reduce.3.cloned.1.call-start = ((), (), s32[]{:S(2)}) async-start(), calls=%async_computation | async-start | bytes 50331648 | tf_op jit(solution)/shard_map/psum | solution.py:30
Sparse Core Ops, SparseCore 0:
  250.8 217.5 all-reduce.4
  471.5 552.2 all-reduce.2
where the time goes:
time: 1050 us
  waiting for transfers between devices  701 us (67%)
  matrix products  203 us (19%)
  other arithmetic  50.3 us (5%)
  blocking collectives  41.7 us (4%)
  local copies, waits for them, and re-layouts  36.8 us (4%)
  between operations  15.9 us (2%)
    psum x1, waiting for transfers between devices, local_step(): dh_student = lax.psum(dh_part, 'tp')  543 us
    psum x1, waiting for transfers between devices, local_step(): dw_student = lax.psum(dw_part, 'dp')  159 us
    dot_general x1, matrix products, local_step(): jnp.dot(h_teacher, w_teacher, preferred_element_type=jnp.float32)  101 us
    unnamed x4, local copies, waits for them, and re-layouts  36.7 us
    dot_general x1, matrix products, local_step(): lax.dot_general(h_student, dz_student, (((0,), (0,)), ((), ())), preferre...  34.1 us
    dot_general x1, matrix products, local_step(): jnp.dot(h_student, w_student, preferred_element_type=jnp.float32)  34 us
    dot_general x1, matrix products, local_step(): lax.dot_general(dz_student, w_student, (((1,), (1,)), ((), ())), preferre...  33.9 us
    convert_element_type x1, other arithmetic, local_step(): dz_student = ((prob_s - prob_t) / tok_total).astype(jnp.bfloat16)  31.6 us
  transfers between devices with their start and end apart: 2, of which 2 were waited for; matrix products, arithmetic and copies ran while one was open for 4% of the time, Pallas kernels for 0%

commit v1 on v0

v1 whole, which is shorter than its diff:
```python
import functools

import jax
import jax.numpy as jnp
from jax import lax
from jax.experimental import pallas as pl
from jax.experimental.pallas import tpu as pltpu
from jax.sharding import PartitionSpec as P

F32 = jnp.float32
BF16 = jnp.bfloat16
VMEM_LIMIT = 67043328
ONCE = pl.Buffered(buffer_count=1)


def params():
    return pltpu.CompilerParams(vmem_limit_bytes=VMEM_LIMIT, dimension_semantics=("arbitrary",))


def cost(flops, nbytes):
    return pl.CostEstimate(flops=int(flops), bytes_accessed=int(nbytes), transcendentals=0)


def lane_fold(x, op):
    acc = x[:, 0:128]
    for j in range(1, x.shape[1] // 128):
        acc = op(acc, x[:, 128 * j:128 * (j + 1)])
    return acc


def logits_body(rows, tile, ht_ref, hs_ref, wt_ref, ws_ref, *rest):
    et_ref, es_ref, stat_ref = rest[-3:]
    block, cols = et_ref.shape
    for r in range(0, block, rows):
        sl = pl.ds(r, rows)
        ht = ht_ref[sl, :]
        hs = hs_ref[sl, :]
        mt = jnp.full((rows, 128), -jnp.inf, F32)
        ms = mt
        for c in range(0, cols, tile):
            zt = jnp.dot(ht, wt_ref[:, c:c + tile], preferred_element_type=F32)
            et_ref[sl, c:c + tile] = zt
            mt = jnp.maximum(mt, lane_fold(zt, jnp.maximum))
            zs = jnp.dot(hs, ws_ref[:, c:c + tile], preferred_element_type=F32)
            es_ref[sl, c:c + tile] = zs
            ms = jnp.maximum(ms, lane_fold(zs, jnp.maximum))
        mt = jnp.max(mt, axis=1, keepdims=True)
        ms = jnp.max(ms, axis=1, keepdims=True)
        st = jnp.zeros((rows, 128), F32)
        ss = st
        dd = st
        for c in range(0, cols, 128):
            xt = et_ref[sl, c:c + 128] - mt
            xs = es_ref[sl, c:c + 128] - ms
            pt = jnp.exp(xt)
            ps = jnp.exp(xs)
            et_ref[sl, c:c + 128] = pt
            es_ref[sl, c:c + 128] = ps
            st = st + pt
            ss = ss + ps
            dd = dd + pt * (xt - xs)
        vals = (mt, jnp.sum(st, axis=1, keepdims=True), ms, jnp.sum(ss, axis=1, keepdims=True),
                jnp.sum(dd, axis=1, keepdims=True))
        lane = lax.broadcasted_iota(jnp.int32, (rows, 128), 1)
        packed = jnp.zeros((rows, 128), F32)
        for i, v in enumerate(vals):
            packed = jnp.where(lane == i, v, packed)
        stat_ref[:, r:r + rows] = jnp.transpose(packed)[0:8, :]


def logits_part(ht, hs, wt, ws, start, count, prev, block=512, rows=256, tile=512):
    tokens, kt = ht.shape
    ks, cols = ws.shape
    first = start // block
    tok = lambda i: (i + first, 0)
    fixed = lambda i: (0, 0)
    in_specs = [pl.BlockSpec((block, kt), tok), pl.BlockSpec((block, ks), tok),
                pl.BlockSpec((kt, cols), fixed, pipeline_mode=ONCE),
                pl.BlockSpec((ks, cols), fixed, pipeline_mode=ONCE)]
    args = [ht, hs, wt, ws]
    alias = {}
    if prev is not None:
        in_specs += [pl.BlockSpec(memory_space=pl.ANY)] * 2
        args += list(prev)
        alias = {4: 0, 5: 1}
    return pl.pallas_call(
        functools.partial(logits_body, rows, tile),
        grid=(count // block,),
        in_specs=in_specs,
        out_specs=[pl.BlockSpec((block, cols), tok), pl.BlockSpec((block, cols), tok),
                   pl.BlockSpec((8, block), lambda i: (0, i))],
        out_shape=[jax.ShapeDtypeStruct((tokens, cols), F32), jax.ShapeDtypeStruct((tokens, cols), F32),
                   jax.ShapeDtypeStruct((8, count), F32)],
        input_output_aliases=alias,
        compiler_params=params(),
        cost_estimate=cost(2 * count * cols * (kt + ks), 2 * cols * (kt + ks) + count * (2 * (kt + ks) + 8 * cols)),
        name="logits",
    )(*args)


def grads_body(hs_ref, ws_ref, et_ref, es_ref, coef_ref, dh_ref, dw_hbm, acc_ref, sem):
    i = pl.program_id(0)
    coef = jnp.transpose(coef_ref[...])
    dz = (es_ref[...] * coef[:, 1:2] - et_ref[...] * coef[:, 0:1]).astype(BF16)
    dh_ref[...] = lax.dot_general(dz, ws_ref[...], (((1,), (1,)), ((), ())), preferred_element_type=F32)
    part = lax.dot_general(hs_ref[...], dz, (((0,), (0,)), ((), ())), preferred_element_type=F32)
    ks = hs_ref.shape[1]
    block = hs_ref.shape[0]

    @pl.when(i == 0)
    def _():
        acc_ref[0:ks, :] = part
        acc_ref[ks:ks + 8, :] = jnp.zeros((8, acc_ref.shape[1]), F32)

    @pl.when(i > 0)
    def _():
        acc_ref[0:ks, :] += part

    acc_ref[ks:ks + 8, 0:block] += coef_ref[...]

    @pl.when(i == pl.num_programs(0) - 1)
    def _():
        copy = pltpu.make_async_copy(acc_ref, dw_hbm, sem)
        copy.start()
        copy.wait()


def grads_part(hs, ws, et, es, coef, block=512):
    tokens, ks = hs.shape
    cols = ws.shape[1]
    tok = lambda i: (i, 0)
    return pl.pallas_call(
        grads_body,
        grid=(tokens // block,),
        in_specs=[pl.BlockSpec((block, ks), tok), pl.BlockSpec((ks, cols), lambda i: (0, 0), pipeline_mode=ONCE),
                  pl.BlockSpec((block, cols), tok), pl.BlockSpec((block, cols), tok),
                  pl.BlockSpec((8, block), lambda i: (0, i))],
        out_specs=[pl.BlockSpec((block, ks), tok), pl.BlockSpec(memory_space=pl.ANY)],
        out_shape=[jax.ShapeDtypeStruct((tokens, ks), F32), jax.ShapeDtypeStruct((ks + 8, cols), F32)],
        scratch_shapes=[pltpu.VMEM((ks + 8, cols), F32), pltpu.SemaphoreType.DMA],
        compiler_params=params(),
        cost_estimate=cost(4 * tokens * cols * ks, 2 * ks * cols + tokens * (6 * ks + 8 * cols) + 4 * ks * cols),
        name="grads",
    )(hs, ws, et, es, coef)


def other_body(npieces, rows, ht_ref, hs_ref, coef_ref, *rest):
    pieces = rest[:npieces]
    dh_in_ref, dh_ref, wt_ref, ws_ref = rest[npieces:]
    kt = ht_ref.shape[1]

    @pl.when(pl.program_id(0) == 0)
    def _():
        at = 0
        for p in pieces:
            w = p.shape[1]
            wt_ref[:, at:at + w] = p[0:kt, :].astype(BF16)
            ws_ref[:, at:at + w] = p[kt:, :].astype(BF16)
            at += w

    for r in range(0, ht_ref.shape[0], rows):
        sl = pl.ds(r, rows)
        coef = jnp.transpose(coef_ref[:, r:r + rows])
        zt = jnp.dot(ht_ref[sl, :], wt_ref[...], preferred_element_type=F32)
        zs = jnp.dot(hs_ref[sl, :], ws_ref[...], preferred_element_type=F32)
        pt = jnp.exp(zt - coef[:, 2:3]) * coef[:, 3:4]
        ps = jnp.exp(zs - coef[:, 4:5]) * coef[:, 5:6]
        dz = (ps - pt).astype(BF16)
        dh_ref[sl, :] = dh_in_ref[sl, :] + lax.dot_general(
            dz, ws_ref[...], (((1,), (1,)), ((), ())), preferred_element_type=F32)


def other_part(ht, hs, coef, pieces, dh, block=512, rows=256):
    tokens, kt = ht.shape
    ks = hs.shape[1]
    cols = sum(p.shape[1] for p in pieces)
    tok = lambda i: (i, 0)
    fixed = lambda i: (0, 0)
    n = len(pieces)
    return pl.pallas_call(
        functools.partial(other_body, n, rows),
        grid=(tokens // block,),
        in_specs=[pl.BlockSpec((block, kt), tok), pl.BlockSpec((block, ks), tok), pl.BlockSpec((8, block), lambda i: (0, i))]
        + [pl.BlockSpec(p.shape, fixed, pipeline_mode=ONCE) for p in pieces]
        + [pl.BlockSpec((block, ks), tok)],
        out_specs=pl.BlockSpec((block, ks), tok),
        out_shape=jax.ShapeDtypeStruct((tokens, ks), F32),
        scratch_shapes=[pltpu.VMEM((kt, cols), BF16), pltpu.VMEM((ks, cols), BF16)],
        input_output_aliases={3 + n: 0},
        compiler_params=params(),
        cost_estimate=cost(2 * tokens * cols * (kt + 2 * ks), 4 * cols * (kt + ks) + tokens * (2 * kt + 10 * ks)),
        name="other",
    )(ht, hs, coef, *pieces, dh)


def solution(mesh):
    dp_size = mesh.shape["dp"]
    swap_tp = [(0, 1), (1, 0)]
    swap_x = [(i, i ^ 2) for i in range(dp_size)]
    swap_core = [(i, i ^ 1) for i in range(dp_size)]

    def local_step(h_teacher, h_student, w_teacher, w_student):
        tokens = h_teacher.shape[0]
        tok_total = tokens * dp_size
        half = tokens // 2
        tp = lax.axis_index("tp")
        dp = lax.axis_index("dp")

        def piece(start, width):
            return jnp.concatenate([lax.dynamic_slice_in_dim(w_teacher, start, width, 1),
                                    lax.dynamic_slice_in_dim(w_student, start, width, 1)], axis=0).astype(F32)

        def over(axis, perm, x):
            return lax.ppermute(x, axis, perm)

        y0 = over("tp", swap_tp, piece(128 * dp, 128))
        y1 = over("tp", swap_tp, piece(512 + 128 * dp, 128))
        et, es, stat_a = logits_part(h_teacher, h_student, w_teacher, w_student, 0, half, None)
        x0 = over("dp", swap_x, y0)
        et, es, stat_b = logits_part(h_teacher, h_student, w_teacher, w_student, half, half, (et, es))
        stat = jnp.concatenate([stat_a, stat_b], axis=1)
        stat_other = over("tp", swap_tp, stat)
        x1 = over("dp", swap_x, y1)

        first = jnp.where(tp == 0, stat, stat_other)
        second = jnp.where(tp == 0, stat_other, stat)
        max_t = jnp.maximum(first[0], second[0])
        max_s = jnp.maximum(first[2], second[2])
        scale_t1, scale_t2 = jnp.exp(first[0] - max_t), jnp.exp(second[0] - max_t)
        scale_s1, scale_s2 = jnp.exp(first[2] - max_s), jnp.exp(second[2] - max_s)
        sum_t = first[1] * scale_t1 + second[1] * scale_t2
        sum_s = first[3] * scale_s1 + second[3] * scale_s2
        inv_t = (1.0 / sum_t) / tok_total
        inv_s = (1.0 / sum_s) / tok_total
        own_t = jnp.exp(stat[0] - max_t) * inv_t
        own_s = jnp.exp(stat[2] - max_s) * inv_s
        num = (scale_t1 * (first[4] + first[1] * ((first[0] - max_t) - (first[2] - max_s)))
               + scale_t2 * (second[4] + second[1] * ((second[0] - max_t) - (second[2] - max_s))))
        kl = num / sum_t - (jnp.log(sum_t) - jnp.log(sum_s))
        coef = jnp.stack([own_t, own_s, max_t, inv_t, max_s, inv_s, kl, jnp.zeros_like(kl)])

        core = dp % 2
        p2, p3, coef = lax.optimization_barrier((piece(1024 + 256 * core, 256), piece(1536 + 256 * core, 256), coef))
        y2 = over("tp", swap_tp, p2)
        y3 = over("tp", swap_tp, p3)
        dh, dw = grads_part(h_student, w_student, et, es, coef)
        dw = lax.psum(dw, "dp")
        cy0 = over("dp", swap_core, y0)
        cx0 = over("dp", swap_core, x0)
        cy1 = over("dp", swap_core, y1)
        cx1 = over("dp", swap_core, x1)
        cy2 = over("dp", swap_core, y2)
        cy3 = over("dp", swap_core, y3)
        for pieces in ((y0, x0, cy0, cx0), (y1, x1, cy1, cx1),
                             (y2, cy2), (y3, cy3)):
            dh = other_part(h_teacher, h_student, coef, pieces, dh)
        depth = h_student.shape[1]
        kl_loss = jnp.sum(dw[depth + 6]) / tok_total
        return kl_loss, dh, dw[0:depth]

    return jax.shard_map(
        local_step, mesh=mesh,
        in_specs=(P("dp", None), P("dp", None), P(None, "tp"), P(None, "tp")),
        out_specs=(P(), P("dp", None), P(None, "tp")),
        check_vma=False)
```

time: 1050 us -> 755 us (0.72)
  waiting for transfers between devices: 701 us -> 312 us
  Pallas kernels: 0 us -> 374 us
  matrix products: 203 us -> 0 us
  other arithmetic: 50.3 us -> 8.08 us
  blocking collectives: 41.7 us -> 0 us
  local copies, waits for them, and re-layouts: 36.8 us -> 24.8 us
  starting transfers between devices: 0.08 us -> 12 us
    psum x2 -> x1, waiting for transfers between devices: 701 us -> 97.5 us  [local_step(): dw = lax.psum(dw, 'dp')]
    pallas_call x0 -> x7, Pallas kernels: none -> 374 us  [the longest x4 173 us: other_part(): pl.pallas_call(functools.partial(other_body, n, rows), grid=(tokens // bl...]
    ppermute x0 -> x13, waiting for transfers between devices: none -> 215 us  [over(): return lax.ppermute(x, axis, perm)]
    dot_general x4 -> x0, matrix products: 203 us -> none  [the longest x1 101 us: local_step(): jnp.dot(h_teacher, w_teacher, preferred_element_type=jnp.float32)]
    unnamed x4 -> x9, local copies, waits for them, and re-layouts: 36.7 us -> 2.71 us
    psum x2 -> x0, blocking collectives: 31.3 us -> none  [the longest x1 24.4 us: local_step(): kl_loss = lax.psum(kl_part, ('tp', 'dp')) / tok_total]
    convert_element_type x1 -> x3, other arithmetic: 31.6 us -> 6.27 us  [piece(): return jnp.concatenate([lax.dynamic_slice_in_dim(w_teacher, start, width,...]
    reduce_sum x2 -> x1, other arithmetic: 18.6 us -> 1.46 us  [local_step(): kl_loss = jnp.sum(dw[depth + 6]) / tok_total]
  transfers between devices with their start and end apart: 2 -> 14, of which waited for: 2 -> 4; matrix products, arithmetic and copies ran while one was open for 4% -> 4% of each run, Pallas kernels for 0% -> 28%
where the time goes in v1:
time: 755 us; the launch traced here: 748 us
  Pallas kernels  374 us (50%)
  waiting for transfers between devices  312 us (41%)
  local copies, waits for them, and re-layouts  24.8 us (3%)
  between operations  16.1 us (2%)
  starting transfers between devices  12 us (2%)
  other arithmetic  8.08 us (1%)
    ppermute x13, waiting for transfers between devices, over(): return lax.ppermute(x, axis, perm)  215 us
    pallas_call x4, Pallas kernels, other_part(): pl.pallas_call(functools.partial(other_body, n, rows), grid=(tokens // bl...  173 us
    pallas_call x2, Pallas kernels, logits_part(): pl.pallas_call(functools.partial(logits_body, rows, tile), grid=(count //...  122 us
    psum x1, waiting for transfers between devices, local_step(): dw = lax.psum(dw, 'dp')  97.5 us
    pallas_call x1, Pallas kernels, grads_part(): pl.pallas_call(grads_body, grid=(tokens // block,), in_specs=[pl.BlockSpe...  79 us
  transfers between devices with their start and end apart: 14, of which 4 were waited for; matrix products, arithmetic and copies ran while one was open for 4% of the time, Pallas kernels for 28%

profile of v1, /device:TPU:0, one launch (start us, length us, event | category | flops | bytes accessed | tf_op | source)
XLA Modules:
  0.0 747.6 jit_solution(1221342691018456662)
XLA Ops:
  7.2 0.0 all-reduce.2.cloned.1.call-start
  7.2 60.6 %logits.2 = (f32[4096,2048]{1,0:T(8,128)}, f32[4096,2048]{1,0:T(8,128)}, f32[8,2048]{1,0:T(8,128)}) custom-call(bf16[4096,3584]{1,0:T(8,128)(2,1)} %ht_ref.11, bf16[4096,1536]{1,0:T(8,128)(2,1)} %hs_ref.13, bf16[3584,2048]{1,0:T(8,128)(2,1)} %wt_ref.3, bf16[1536,2048]{1,0:T(8,128)(2,1)} %ws_ref.5), custom_call_target="tpu_custom_call" | custom-call | flops 42949672960 | bytes 75497472 | tf_op jit(solution)/shard_map/logits/pallas_call | solution.py:86
  67.8 1.5 constant_dynamic-update-slice_fusion.1
  69.3 61.4 %logits.3 = (f32[4096,2048]{1,0:T(8,128)}, f32[4096,2048]{1,0:T(8,128)}, f32[8,2048]{1,0:T(8,128)}) custom-call(bf16[4096,3584]{1,0:T(8,128)(2,1)} %ht_ref.11, bf16[4096,1536]{1,0:T(8,128)(2,1)} %hs_ref.13, bf16[3584,2048]{1,0:T(8,128)(2,1)} %wt_ref.3, bf16[1536,2048]{1,0:T(8,128)(2,1)} %ws_ref.5, ...), custom_call_target="tpu_custom_call", output_to_operand_aliasing={{0}: (4, {}), {1}: (5, {})} | custom-call | flops 42949672960 | bytes 75497472 | tf_op jit(solution)/shard_map/logits/pallas_call | solution.py:86
  130.7 1.5 constant_dynamic-update-slice_fusion
  132.1 3.3 collective-permute-start
  135.5 2.5 constant_dynamic-slice_fusion.1
  138.0 1.9 constant_dynamic-slice_fusion
  140.0 1.7 maximum_convert_fusion.3
  141.6 0.0 collective-permute-start.9
  141.6 2.3 constant_dynamic-slice_fusion.5
  143.9 1.5 constant_dynamic-slice_fusion.4
  145.4 0.0 copy-start.2
  145.4 4.4 maximum_convert_fusion
  149.9 0.0 collective-permute-done
  149.9 0.0 copy-done.2
  149.9 0.2 subtract_subtract_fusion
  150.1 0.1 fusion.5
  150.3 0.8 stack.2.coef_ref
  151.1 79.0 %grads.1 = (f32[4096,1536]{1,0:T(8,128)}, f32[1544,2048]{1,0:T(8,128)}) custom-call(bf16[4096,1536]{1,0:T(8,128)(2,1)} %hs_ref.13, bf16[1536,2048]{1,0:T(8,128)(2,1)} %ws_ref.5, f32[4096,2048]{1,0:T(8,128)} %get-tuple-element.16.et_ref, f32[4096,2048]{1,0:T(8,128)} %get-tuple-element.17.es_ref, f32[8,4096]{1,0:T(8,128)} %stack.2.coef_ref), custom_call_target="tpu_custom_call" | custom-call | flops 51539607552 | bytes 123731968 | tf_op jit(solution)/shard_map/grads/pallas_call | solution.py:132
  230.1 0.0 copy-start
  230.1 0.0 copy-start.1
  230.1 0.0 all-reduce.2.cloned.1.call-update
  230.1 1.1 copy-done
  231.3 0.1 copy-done.1
  231.3 0.2 maximum_convert_fusion.2
  231.5 2.1 collective-permute-start.5
  233.6 0.0 collective-permute-start.3
  233.7 2.0 collective-permute-start.1
  235.7 0.0 collective-permute-done.9.rest_0_
  235.7 1.5 collective-permute-start.10
  237.1 0.0 collective-permute-start.11
  237.1 54.3 %collective-permute-done.5.rest_0_ = f32[5120,128]{1,0:T(8,128)} collective-permute-done((f32[5120,128]{1,0:T(8,128)S(1)}, f32[5120,128]{1,0:T(8,128)}, u32[]{:S(2)}, u32[]{:S(2)}) %collective-permute-start.5) | collective-permute-done | bytes 2621472 | tf_op jit(solution)/shard_map/ppermute | solution.py:214
  291.4 2.0 collective-permute-start.6
  293.4 58.3 %collective-permute-done.10.rest_1_ = f32[5120,128]{1,0:T(8,128)S(1)} collective-permute-done((f32[5120,128]{1,0:T(8,128)}, f32[5120,128]{1,0:T(8,128)S(1)}, u32[]{:S(2)}, u32[]{:S(2)}) %collective-permute-start.10) | collective-permute-done | bytes 2621472 | tf_op jit(solution)/shard_map/ppermute | solution.py:214
  351.8 0.0 copy-start.3
  351.8 0.0 collective-permute-start.12
  351.8 0.0 collective-permute-done.11.rest_2_
  351.8 0.5 collective-permute-start.7
  352.3 102.0 %collective-permute-done.6.rest_1_ = f32[5120,128]{1,0:T(8,128)} collective-permute-done((f32[5120,128]{1,0:T(8,128)}, f32[5120,128]{1,0:T(8,128)}, u32[]{:S(2)}, u32[]{:S(2)}) %collective-permute-start.6) | collective-permute-done | bytes 2621472 | tf_op jit(solution)/shard_map/ppermute | solution.py:214
  454.3 0.0 collective-permute-start.8
  454.3 0.0 collective-permute-done.3.rest_0_
  454.3 0.5 collective-permute-start.4
  454.8 97.5 %all-reduce.2.cloned.1.call-done = f32[1544,2048]{1,0:T(8,128)} async-done(((f32[1544,2048]{1,0:T(8,128)}), f32[1544,2048]{1,0:T(8,128)}) %all-reduce.2.cloned.1.call-update) | async-done | bytes 12648464 | tf_op jit(solution)/shard_map/psum | solution.py:247
  552.4 1.5 slice_reduce_fusion
  554.5 11.5 %slice.79 = f32[1536,2048]{1,0:T(8,128)} slice(f32[1544,2048]{1,0:T(8,128)} %all-reduce.2.cloned.1.call-done), slice={[0:1536], [0:2048]} | slice | bytes 25165824 | tf_op jit(solution)/shard_map/slice | solution.py:259
  566.0 0.0 copy-done.3
  566.0 0.0 collective-permute-done.1.rest_0_
  566.0 0.0 collective-permute-start.2
  566.0 0.0 collective-permute-done.12.rest_3_
  566.1 43.6 %other.4.rest_4_ = f32[4096,1536]{1,0:T(8,128)} custom-call(bf16[4096,3584]{1,0:T(8,128)(2,1)} %ht_ref.11, bf16[4096,1536]{1,0:T(8,128)(2,1)} %hs_ref.13, f32[8,4096]{1,0:T(8,128)} %stack.2.coef_ref, f32[5120,128]{1,0:T(8,128)} %collective-permute-done.9.rest_0_, f32[5120,128]{1,0:T(8,128)} %copy-done.3, ...), custom_call_target="tpu_custom_call", output_to_operand_aliasing={{}: (7, {})} | custom-call | flops 27917287424 | bytes 102760448 | tf_op jit(solution)/shard_map/other/pallas_call | solution.py:180
  609.6 0.0 collective-permute-done.7.rest_2_
  609.7 0.0 collective-permute-done.8.rest_3_
  609.7 43.3 %other.5.rest_2_ = f32[4096,1536]{1,0:T(8,128)} custom-call(bf16[4096,3584]{1,0:T(8,128)(2,1)} %ht_ref.11, bf16[4096,1536]{1,0:T(8,128)(2,1)} %hs_ref.13, f32[8,4096]{1,0:T(8,128)} %stack.2.coef_ref, f32[5120,128]{1,0:T(8,128)} %collective-permute-done.5.rest_0_, f32[5120,128]{1,0:T(8,128)} %collective-permute-done.6.rest_1_, ...), custom_call_target="tpu_custom_call", output_to_operand_aliasing={{}: (7, {})} | custom-call | flops 27917287424 | bytes 102760448 | tf_op jit(solution)/shard_map/other/pallas_call | solution.py:180
  653.0 0.0 collective-permute-done.4.rest_1_
  653.0 43.0 %other.6.rest_2_ = f32[4096,1536]{1,0:T(8,128)} custom-call(bf16[4096,3584]{1,0:T(8,128)(2,1)} %ht_ref.11, bf16[4096,1536]{1,0:T(8,128)(2,1)} %hs_ref.13, f32[8,4096]{1,0:T(8,128)} %stack.2.coef_ref, f32[5120,256]{1,0:T(8,128)} %collective-permute-done.3.rest_0_, f32[5120,256]{1,0:T(8,128)} %collective-permute-done.4.rest_1_, ...), custom_call_target="tpu_custom_call", output_to_operand_aliasing={{}: (5, {})} | custom-call | flops 27917287424 | bytes 102760448 | tf_op jit(solution)/shard_map/other/pallas_call | solution.py:180
  696.0 0.0 collective-permute-done.2.rest_1_
  696.0 43.5 %other.7 = f32[4096,1536]{1,0:T(8,128)} custom-call(bf16[4096,3584]{1,0:T(8,128)(2,1)} %ht_ref.11, bf16[4096,1536]{1,0:T(8,128)(2,1)} %hs_ref.13, f32[8,4096]{1,0:T(8,128)} %stack.2.coef_ref, f32[5120,256]{1,0:T(8,128)} %collective-permute-done.1.rest_0_, f32[5120,256]{1,0:T(8,128)} %collective-permute-done.2.rest_1_, ...), custom_call_target="tpu_custom_call", output_to_operand_aliasing={{}: (5, {})} | custom-call | flops 27917287424 | bytes 102760448 | tf_op jit(solution)/shard_map/other/pallas_call | solution.py:180
  (2 shorter events, 0.0 us)
Async XLA Ops:
  7.2 545.2 %all-reduce.2.cloned.1.call-start = ((), (), s32[]{:S(2)}) async-start(), calls=%async_computation | async-start | bytes 25296896 | tf_op jit(solution)/shard_map/psum | solution.py:247
  132.1 17.7 %collective-permute-start = (f32[8,4096]{1,0:T(8,128)}, f32[8,4096]{1,0:T(8,128)S(1)}, u32[]{:S(2)}, u32[]{:S(2)}) collective-permute-start(f32[8,4096]{1,0:T(8,128)} %constant_dynamic-update-slice_fusion), channel_id=1, source_target_pairs={{0,4},{4,0},{1,5},{5,1},{2,6},{6,2},{3,7},{7,3}} | collective-permute-start | bytes 393224 | tf_op jit(solution)/shard_map/ppermute | solution.py:214
  141.6 94.0 %collective-permute-start.9 = (f32[5120,128]{1,0:T(8,128)}, f32[5120,128]{1,0:T(8,128)}, u32[]{:S(2)}, u32[]{:S(2)}) collective-permute-start(f32[5120,128]{1,0:T(8,128)} %maximum_convert_fusion.3), channel_id=1, source_target_pairs={{0,4},{4,0},{1,5},{5,1},{2,6},{6,2},{3,7},{7,3}} | collective-permute-start | bytes 7864328 | tf_op jit(solution)/shard_map/ppermute | solution.py:214
  145.4 4.5 copy-start.2
  230.1 1.2 copy-start
  230.1 1.3 copy-start.1
  231.5 59.9 %collective-permute-start.5 = (f32[5120,128]{1,0:T(8,128)S(1)}, f32[5120,128]{1,0:T(8,128)}, u32[]{:S(2)}, u32[]{:S(2)}) collective-permute-start(f32[5120,128]{1,0:T(8,128)S(1)} %maximum_convert_fusion.2), channel_id=1, source_target_pairs={{0,4},{4,0},{1,5},{5,1},{2,6},{6,2},{3,7},{7,3}} | collective-permute-start | bytes 7864328 | tf_op jit(solution)/shard_map/ppermute | solution.py:214
  233.6 220.7 %collective-permute-start.3 = (f32[5120,256]{1,0:T(8,128)}, f32[5120,256]{1,0:T(8,128)}, u32[]{:S(2)}, u32[]{:S(2)}) collective-permute-start(f32[5120,256]{1,0:T(8,128)} %get-tuple-element.23), channel_id=1, source_target_pairs={{0,4},{4,0},{1,5},{5,1},{2,6},{6,2},{3,7},{7,3}} | collective-permute-start | bytes 15728648 | tf_op jit(solution)/shard_map/ppermute | solution.py:214
  233.7 332.4 %collective-permute-start.1 = (f32[5120,256]{1,0:T(8,128)}, f32[5120,256]{1,0:T(8,128)}, u32[]{:S(2)}, u32[]{:S(2)}) collective-permute-start(f32[5120,256]{1,0:T(8,128)} %get-tuple-element.22), channel_id=1, source_target_pairs={{0,4},{4,0},{1,5},{5,1},{2,6},{6,2},{3,7},{7,3}} | collective-permute-start | bytes 15728648 | tf_op jit(solution)/shard_map/ppermute | solution.py:214
  235.7 116.1 %collective-permute-start.10 = (f32[5120,128]{1,0:T(8,128)}, f32[5120,128]{1,0:T(8,128)S(1)}, u32[]{:S(2)}, u32[]{:S(2)}) collective-permute-start(f32[5120,128]{1,0:T(8,128)} %collective-permute-done.9.rest_0_), channel_id=1, source_target_pairs={{0,2},{1,3},{2,0},{3,1},{4,6},{5,7},{6,4},{7,5}} | collective-permute-start | bytes 7864328 | tf_op jit(solution)/shard_map/ppermute | solution.py:214
  237.1 114.6 %collective-permute-start.11 = (f32[5120,128]{1,0:T(8,128)}, f32[5120,128]{1,0:T(8,128)}, u32[]{:S(2)}, u32[]{:S(2)}) collective-permute-start(f32[5120,128]{1,0:T(8,128)} %collective-permute-done.9.rest_0_), channel_id=1, source_target_pairs={{0,1},{1,0},{2,3},{3,2},{4,5},{5,4},{6,7},{7,6}} | collective-permute-start | bytes 7864328 | tf_op jit(solution)/shard_map/ppermute | solution.py:214
  291.4 162.9 %collective-permute-start.6 = (f32[5120,128]{1,0:T(8,128)}, f32[5120,128]{1,0:T(8,128)}, u32[]{:S(2)}, u32[]{:S(2)}) collective-permute-start(f32[5120,128]{1,0:T(8,128)} %collective-permute-done.5.rest_0_), channel_id=1, source_target_pairs={{0,2},{1,3},{2,0},{3,1},{4,6},{5,7},{6,4},{7,5}} | collective-permute-start | bytes 7864328 | tf_op jit(solution)/shard_map/ppermute | solution.py:214
  351.8 214.3 %copy-start.3 = (f32[5120,128]{1,0:T(8,128)}, f32[5120,128]{1,0:T(8,128)S(1)}, u32[]{:S(2)}) copy-start(f32[5120,128]{1,0:T(8,128)S(1)} %collective-permute-done.10.rest_1_) | copy-start | bytes 7864324
  351.8 214.3 %collective-permute-start.12 = (f32[5120,128]{1,0:T(8,128)S(1)}, f32[5120,128]{1,0:T(8,128)}, u32[]{:S(2)}, u32[]{:S(2)}) collective-permute-start(f32[5120,128]{1,0:T(8,128)S(1)} %collective-permute-done.10.rest_1_), channel_id=1, source_target_pairs={{0,1},{1,0},{2,3},{3,2},{4,5},{5,4},{6,7},{7,6}} | collective-permute-start | bytes 7864328 | tf_op jit(solution)/shard_map/ppermute | solution.py:214
  351.8 257.9 %collective-permute-start.7 = (f32[5120,128]{1,0:T(8,128)}, f32[5120,128]{1,0:T(8,128)}, u32[]{:S(2)}, u32[]{:S(2)}) collective-permute-start(f32[5120,128]{1,0:T(8,128)} %collective-permute-done.5.rest_0_), channel_id=1, source_target_pairs={{0,1},{1,0},{2,3},{3,2},{4,5},{5,4},{6,7},{7,6}} | collective-permute-start | bytes 7864328 | tf_op jit(solution)/shard_map/ppermute | solution.py:214
  454.3 155.3 %collective-permute-start.8 = (f32[5120,128]{1,0:T(8,128)}, f32[5120,128]{1,0:T(8,128)}, u32[]{:S(2)}, u32[]{:S(2)}) collective-permute-start(f32[5120,128]{1,0:T(8,128)} %collective-permute-done.6.rest_1_), channel_id=1, source_target_pairs={{0,1},{1,0},{2,3},{3,2},{4,5},{5,4},{6,7},{7,6}} | collective-permute-start | bytes 7864328 | tf_op jit(solution)/shard_map/ppermute | solution.py:214
  454.3 198.7 %collective-permute-start.4 = (f32[5120,256]{1,0:T(8,128)}, f32[5120,256]{1,0:T(8,128)}, u32[]{:S(2)}, u32[]{:S(2)}) collective-permute-start(f32[5120,256]{1,0:T(8,128)} %collective-permute-done.3.rest_0_), channel_id=1, source_target_pairs={{0,1},{1,0},{2,3},{3,2},{4,5},{5,4},{6,7},{7,6}} | collective-permute-start | bytes 15728648 | tf_op jit(solution)/shard_map/ppermute | solution.py:214
  566.0 130.0 %collective-permute-start.2 = (f32[5120,256]{1,0:T(8,128)}, f32[5120,256]{1,0:T(8,128)}, u32[]{:S(2)}, u32[]{:S(2)}) collective-permute-start(f32[5120,256]{1,0:T(8,128)} %collective-permute-done.1.rest_0_), channel_id=1, source_target_pairs={{0,1},{1,0},{2,3},{3,2},{4,5},{5,4},{6,7},{7,6}} | collective-permute-start | bytes 15728648 | tf_op jit(solution)/shard_map/ppermute | solution.py:214
Sparse Core Ops, SparseCore 0:
  230.2 322.0 all-reduce.1

commit v2 on v1

v2 whole, which is shorter than its diff:
```python
import functools

import jax
import jax.numpy as jnp
from jax import lax
from jax.experimental import pallas as pl
from jax.experimental.pallas import tpu as pltpu
from jax.sharding import PartitionSpec as P

F32 = jnp.float32
BF16 = jnp.bfloat16
VMEM_LIMIT = 67043328
ONCE = pl.Buffered(buffer_count=1)


def params():
    return pltpu.CompilerParams(vmem_limit_bytes=VMEM_LIMIT, dimension_semantics=("arbitrary",))


def cost(flops, nbytes):
    return pl.CostEstimate(flops=int(flops), bytes_accessed=int(nbytes), transcendentals=0)


def lane_fold(x, op):
    acc = x[:, 0:128]
    for j in range(1, x.shape[1] // 128):
        acc = op(acc, x[:, 128 * j:128 * (j + 1)])
    return acc


def logits_body(tile, ht_ref, hs_ref, wt_ref, ws_ref, *rest):
    et_ref, es_ref, stat_ref = rest[-3:]
    rows, cols = et_ref.shape
    low = jnp.full((rows, 128), -jnp.inf, F32)

    def products(c, carry):
        mt, ms = carry
        at = pl.ds(pl.multiple_of(c * tile, tile), tile)
        zt = jnp.dot(ht_ref[...], wt_ref[:, at], preferred_element_type=F32)
        et_ref[:, at] = zt
        mt = jnp.maximum(mt, lane_fold(zt, jnp.maximum))
        zs = jnp.dot(hs_ref[...], ws_ref[:, at], preferred_element_type=F32)
        es_ref[:, at] = zs
        return mt, jnp.maximum(ms, lane_fold(zs, jnp.maximum))

    mt, ms = lax.fori_loop(0, cols // tile, products, (low, low))
    mt = jnp.max(mt, axis=1, keepdims=True)
    ms = jnp.max(ms, axis=1, keepdims=True)
    zero = jnp.zeros((rows, 128), F32)
    step = 256

    def exps(c, carry):
        st, ss, dd = carry
        at = pl.ds(pl.multiple_of(c * step, step), step)
        xt = et_ref[:, at] - mt
        xs = es_ref[:, at] - ms
        pt = jnp.exp(xt)
        ps = jnp.exp(xs)
        et_ref[:, at] = pt
        es_ref[:, at] = ps
        return st + lane_fold(pt, jnp.add), ss + lane_fold(ps, jnp.add), dd + lane_fold(pt * (xt - xs), jnp.add)

    st, ss, dd = lax.fori_loop(0, cols // step, exps, (zero, zero, zero))
    vals = (mt, jnp.sum(st, axis=1, keepdims=True), ms, jnp.sum(ss, axis=1, keepdims=True),
            jnp.sum(dd, axis=1, keepdims=True))
    lane = lax.broadcasted_iota(jnp.int32, (rows, 128), 1)
    packed = zero
    for i, v in enumerate(vals):
        packed = jnp.where(lane == i, v, packed)
    stat_ref[...] = jnp.transpose(packed)[0:8, :]


def logits_part(ht, hs, wt, ws, start, count, prev, block=512, tile=512):
    tokens, kt = ht.shape
    ks, cols = ws.shape
    first = start // block
    tok = lambda i: (i + first, 0)
    fixed = lambda i: (0, 0)
    in_specs = [pl.BlockSpec((block, kt), tok), pl.BlockSpec((block, ks), tok),
                pl.BlockSpec((kt, cols), fixed, pipeline_mode=ONCE),
                pl.BlockSpec((ks, cols), fixed, pipeline_mode=ONCE)]
    args = [ht, hs, wt, ws]
    alias = {}
    if prev is not None:
        in_specs += [pl.BlockSpec(memory_space=pl.ANY)] * 2
        args += list(prev)
        alias = {4: 0, 5: 1}
    return pl.pallas_call(
        functools.partial(logits_body, tile),
        grid=(count // block,),
        in_specs=in_specs,
        out_specs=[pl.BlockSpec((block, cols), tok), pl.BlockSpec((block, cols), tok),
                   pl.BlockSpec((8, block), lambda i: (0, i))],
        out_shape=[jax.ShapeDtypeStruct((tokens, cols), F32), jax.ShapeDtypeStruct((tokens, cols), F32),
                   jax.ShapeDtypeStruct((8, count), F32)],
        input_output_aliases=alias,
        compiler_params=params(),
        cost_estimate=cost(2 * count * cols * (kt + ks), 2 * cols * (kt + ks) + count * (2 * (kt + ks) + 8 * cols)),
        name="logits",
    )(*args)


def grads_body(core_ref, hs_ref, ws_ref, et_ref, es_ref, coef_ref, dh_ref, mine_hbm, theirs_hbm, acc_ref, sem):
    i = pl.program_id(0)
    core = core_ref[0]
    block, ks = hs_ref.shape
    width = acc_ref.shape[2]

    @pl.when(i == 0)
    def _():
        acc_ref[...] = jnp.zeros(acc_ref.shape, F32)

    coef = jnp.transpose(coef_ref[...])
    dz = (es_ref[...] * coef[:, 1:2] - et_ref[...] * coef[:, 0:1]).astype(BF16)
    dh_ref[...] = lax.dot_general(dz, ws_ref[...], (((1,), (1,)), ((), ())), preferred_element_type=F32)
    hs_t = jnp.transpose(hs_ref[...])
    for c in range(0, 2 * width, 512):
        half, at = c // width, c % width
        acc_ref[half, 0:ks, at:at + 512] += jnp.dot(hs_t, dz[:, c:c + 512], preferred_element_type=F32)
    for half in range(2):
        acc_ref[half, ks:ks + 8, 0:block] += coef_ref[...]

    @pl.when(i == pl.num_programs(0) - 1)
    def _():
        first = pltpu.make_async_copy(acc_ref.at[1 - core], theirs_hbm, sem.at[0])
        second = pltpu.make_async_copy(acc_ref.at[core], mine_hbm, sem.at[1])
        first.start()
        second.start()
        first.wait()
        second.wait()


def grads_part(core, hs, ws, et, es, coef, block=512):
    tokens, ks = hs.shape
    cols = ws.shape[1]
    tok = lambda i, c: (i, 0)
    half = jax.ShapeDtypeStruct((ks + 8, cols // 2), F32)
    return pl.pallas_call(
        grads_body,
        grid_spec=pltpu.PrefetchScalarGridSpec(
            num_scalar_prefetch=1,
            grid=(tokens // block,),
            in_specs=[pl.BlockSpec((block, ks), tok), pl.BlockSpec((ks, cols), lambda i, c: (0, 0), pipeline_mode=ONCE),
                      pl.BlockSpec((block, cols), tok), pl.BlockSpec((block, cols), tok),
                      pl.BlockSpec((8, block), lambda i, c: (0, i))],
            out_specs=[pl.BlockSpec((block, ks), tok), pl.BlockSpec(memory_space=pl.ANY),
                       pl.BlockSpec(memory_space=pl.ANY)],
            scratch_shapes=[pltpu.VMEM((2, ks + 8, cols // 2), F32), pltpu.SemaphoreType.DMA((2,))]),
        out_shape=[jax.ShapeDtypeStruct((tokens, ks), F32), half, half],
        compiler_params=params(),
        cost_estimate=cost(4 * tokens * cols * ks, 2 * ks * cols + tokens * (6 * ks + 8 * cols) + 4 * ks * cols),
        name="grads",
    )(core, hs, ws, et, es, coef)


def other_body(kinds, rows, ht_ref, hs_ref, coef_ref, *rest):
    pieces = rest[:len(kinds)]
    dh_in_ref, dh_ref, wt_ref, ws_ref = rest[len(kinds):]
    kt = ht_ref.shape[1]

    @pl.when(pl.program_id(0) == 0)
    def _():
        at_t = at_s = 0
        for kind, p in zip(kinds, pieces):
            w = p.shape[1]
            if "t" in kind:
                wt_ref[:, at_t:at_t + w] = p[0:kt, :].astype(BF16)
                at_t += w
            if "s" in kind:
                ws_ref[:, at_s:at_s + w] = p[p.shape[0] - ws_ref.shape[0]:, :].astype(BF16)
                at_s += w

    for r in range(0, ht_ref.shape[0], rows):
        sl = pl.ds(r, rows)
        coef = jnp.transpose(coef_ref[:, r:r + rows])
        zt = jnp.dot(ht_ref[sl, :], wt_ref[...], preferred_element_type=F32)
        zs = jnp.dot(hs_ref[sl, :], ws_ref[...], preferred_element_type=F32)
        pt = jnp.exp(zt - coef[:, 2:3]) * coef[:, 3:4]
        ps = jnp.exp(zs - coef[:, 4:5]) * coef[:, 5:6]
        dz = (ps - pt).astype(BF16)
        dh_ref[sl, :] = dh_in_ref[sl, :] + lax.dot_general(
            dz, ws_ref[...], (((1,), (1,)), ((), ())), preferred_element_type=F32)


def other_part(ht, hs, coef, pieces, dh, block=512, rows=512):
    tokens, kt = ht.shape
    ks = hs.shape[1]
    kinds = tuple(k for k, _ in pieces)
    arrays = [p for _, p in pieces]
    cols = sum(p.shape[1] for k, p in pieces if "t" in k)
    tok = lambda i: (i, 0)
    fixed = lambda i: (0, 0)
    n = len(pieces)
    return pl.pallas_call(
        functools.partial(other_body, kinds, rows),
        grid=(tokens // block,),
        in_specs=[pl.BlockSpec((block, kt), tok), pl.BlockSpec((block, ks), tok), pl.BlockSpec((8, block), lambda i: (0, i))]
        + [pl.BlockSpec(p.shape, fixed, pipeline_mode=ONCE) for p in arrays]
        + [pl.BlockSpec((block, ks), tok)],
        out_specs=pl.BlockSpec((block, ks), tok),
        out_shape=jax.ShapeDtypeStruct((tokens, ks), F32),
        scratch_shapes=[pltpu.VMEM((kt, cols), BF16), pltpu.VMEM((ks, cols), BF16)],
        input_output_aliases={3 + n: 0},
        compiler_params=params(),
        cost_estimate=cost(2 * tokens * cols * (kt + 2 * ks), 4 * cols * (kt + ks) + tokens * (2 * kt + 10 * ks)),
        name="other",
    )(ht, hs, coef, *arrays, dh)


def cast_part(weights, blocks):
    depth = sum(w.shape[0] for w in weights)

    def body(at_ref, *refs):
        row = 0
        for ref in refs[:-1]:
            refs[-1][row:row + ref.shape[0], :] = ref[...].astype(F32)
            row += ref.shape[0]

    return pl.pallas_call(
        body,
        grid_spec=pltpu.PrefetchScalarGridSpec(
            num_scalar_prefetch=1,
            grid=(len(blocks),),
            in_specs=[pl.BlockSpec((w.shape[0], 128), lambda i, at: (0, at[i])) for w in weights],
            out_specs=pl.BlockSpec((depth, 128), lambda i, at: (0, i))),
        out_shape=jax.ShapeDtypeStruct((depth, 128 * len(blocks)), F32),
        compiler_params=params(),
        cost_estimate=cost(128 * depth, 768 * depth * len(blocks)),
        name="cast",
    )(jnp.stack(blocks).astype(jnp.int32), *weights)


def total_part(half, a, b, row, rows, shape, prev=None, block=384):
    width = shape[1] // 2

    def body(half_ref, a_ref, b_ref, *rest):
        rest[-1][...] = a_ref[...] + b_ref[...]

    here = lambda i, h: (i, 0)
    return pl.pallas_call(
        body,
        grid_spec=pltpu.PrefetchScalarGridSpec(
            num_scalar_prefetch=1,
            grid=(rows // block,),
            in_specs=[pl.BlockSpec((block, width), here), pl.BlockSpec((block, width), here)]
            + ([] if prev is None else [pl.BlockSpec(memory_space=pl.ANY)]),
            out_specs=pl.BlockSpec((block, width), lambda i, h: (i + row // block, h[0]))),
        out_shape=jax.ShapeDtypeStruct(shape, F32),
        input_output_aliases={} if prev is None else {3: 0},
        compiler_params=params(),
        cost_estimate=cost(rows * width, 12 * rows * width),
        name="total",
    )(half, a, b, *(() if prev is None else (prev,)))


def solution(mesh):
    dp_size = mesh.shape["dp"]
    swap_tp = [(0, 1), (1, 0)]
    swap_x = [(i, i ^ 2) for i in range(dp_size)]
    swap_core = [(i, i ^ 1) for i in range(dp_size)]

    def local_step(h_teacher, h_student, w_teacher, w_student):
        tokens, depth = h_student.shape
        tok_total = tokens * dp_size
        half = tokens // 2
        tp = lax.axis_index("tp")
        dp = lax.axis_index("dp")
        core, x = dp % 2, dp // 2
        both = (w_teacher, w_student)
        quarter, beside = 2 * core + x, 2 * core + 1 - x

        def over(axis, perm, v):
            return lax.ppermute(v, axis, perm)

        def to_tp(v):
            return over("tp", swap_tp, v)

        def to_x(v):
            return over("dp", swap_x, v)

        def to_core(v):
            return over("dp", swap_core, v)

        y0 = to_tp(cast_part(both, [quarter]))
        y1 = to_tp(cast_part(both, [4 + quarter]))
        et, es, stat_a = logits_part(h_teacher, h_student, w_teacher, w_student, 0, half, None)
        x0 = to_x(y0)
        et, es, stat_b = logits_part(h_teacher, h_student, w_teacher, w_student, half, half, (et, es))
        stat = jnp.concatenate([stat_a, stat_b], axis=1)
        stat_other = to_tp(stat)
        x1 = to_x(y1)

        first = jnp.where(tp == 0, stat, stat_other)
        second = jnp.where(tp == 0, stat_other, stat)
        max_t = jnp.maximum(first[0], second[0])
        max_s = jnp.maximum(first[2], second[2])
        scale_t1, scale_t2 = jnp.exp(first[0] - max_t), jnp.exp(second[0] - max_t)
        scale_s1, scale_s2 = jnp.exp(first[2] - max_s), jnp.exp(second[2] - max_s)
        sum_t = first[1] * scale_t1 + second[1] * scale_t2
        sum_s = first[3] * scale_s1 + second[3] * scale_s2
        inv_t = (1.0 / sum_t) / tok_total
        inv_s = (1.0 / sum_s) / tok_total
        own_t = jnp.exp(stat[0] - max_t) * inv_t
        own_s = jnp.exp(stat[2] - max_s) * inv_s
        num = (scale_t1 * (first[4] + first[1] * ((first[0] - max_t) - (first[2] - max_s)))
               + scale_t2 * (second[4] + second[1] * ((second[0] - max_t) - (second[2] - max_s))))
        kl = num / sum_t - (jnp.log(sum_t) - jnp.log(sum_s))
        coef = jnp.stack([own_t, own_s, max_t, inv_t, max_s, inv_s, kl, jnp.zeros_like(kl)])

        casts = (cast_part((w_student,), [8 + quarter]), cast_part((w_teacher,), [8 + quarter, 8 + beside]),
                 cast_part(both, [12 + core]), cast_part(both, [14 + core]))
        casts, coef = lax.optimization_barrier((casts, coef))
        y2s = to_tp(casts[0])
        y2t = to_tp(casts[1])
        y3 = to_tp(casts[2])
        y4 = to_tp(casts[3])
        core_at = jnp.reshape(core, (1,)).astype(jnp.int32)
        dh, mine, theirs = grads_part(core_at, h_student, w_student, et, es, coef)
        got = to_core(theirs)
        cy0, cx0 = to_core(y0), to_core(x0)
        cy1, cx1 = to_core(y1), to_core(x1)
        x2s = to_x(y2s)
        cy2s, cx2s, cy2t = to_core(y2s), to_core(x2s), to_core(y2t)
        cy3, cy4 = to_core(y3), to_core(y4)

        cut = depth // 2
        chip_a, chip_b = mine[0:cut] + got[0:cut], mine[cut:] + got[cut:]
        far_a, far_b = to_x(chip_a), to_x(chip_b)
        beside_a, beside_b = to_core(chip_a), to_core(chip_b)
        cross_a, cross_b = to_core(far_a), to_core(far_b)

        for pieces in ((("ts", y0), ("ts", x0), ("ts", cy0), ("ts", cx0)),
                             (("ts", y1), ("ts", x1), ("ts", cy1), ("ts", cx1)),
                             (("t", y2t), ("t", cy2t), ("s", y2s), ("s", x2s), ("s", cy2s), ("s", cx2s)),
                             (("ts", y3), ("ts", cy3)),
                             (("ts", y4), ("ts", cy4))):
            dh = other_part(h_teacher, h_student, coef, pieces, dh)

        shape = w_student.shape
        dw = total_part(core_at, chip_a, far_a, 0, cut, shape)
        dw = total_part(1 - core_at, beside_a, cross_a, 0, cut, shape, dw)
        dw = total_part(core_at, chip_b, far_b, cut, cut, shape, dw)
        dw = total_part(1 - core_at, beside_b, cross_b, cut, cut, shape, dw)
        kl_loss = jnp.sum(chip_b[cut + 6] + far_b[cut + 6]) / tok_total
        return kl_loss, dh, dw

    return jax.shard_map(
        local_step, mesh=mesh,
        in_specs=(P("dp", None), P("dp", None), P(None, "tp"), P(None, "tp")),
        out_specs=(P(), P("dp", None), P(None, "tp")),
        check_vma=False)
```

time: 755 us -> 806 us (1.068)
  Pallas kernels: 374 us -> 452 us
  local copies, waits for them, and re-layouts: 24.8 us -> 5.08 us
  between operations: 16.1 us -> 2.59 us
    ppermute x13 -> x26, waiting for transfers between devices: 215 us -> 315 us  [over(): return lax.ppermute(v, axis, perm)]
    psum x1 -> x0, waiting for transfers between devices: 97.5 us -> none  [local_step(): dw = lax.psum(dw, 'dp')]
    pallas_call x7 -> x18, Pallas kernels: 374 us -> 452 us  [the longest x5 206 us: other_part(): pl.pallas_call(functools.partial(other_body, kinds, rows), grid=(tokens /...]
    slice x1 -> x0, local copies, waits for them, and re-layouts: 11.5 us -> none  [local_step(): return (kl_loss, dh, dw[0:depth])]
    add x0 -> x2, other arithmetic: none -> 10.2 us  [local_step(): chip_a, chip_b = (mine[0:cut] + got[0:cut], mine[cut:] + got[cut:])]
    dynamic_slice x4 -> x0, local copies, waits for them, and re-layouts: 8.27 us -> none  [the longest x2 4.83 us: piece(): lax.dynamic_slice_in_dim(w_teacher, start, width, 1)]
  transfers between devices with their start and end apart: 14 -> 26, of which waited for: 4 -> 8; matrix products, arithmetic and copies ran while one was open for 4% -> 2% of each run, Pallas kernels for 28% -> 29%
where the time goes in v2:
time: 806 us; the launch traced here: 805 us
  Pallas kernels  452 us (56%)
  waiting for transfers between devices  315 us (39%)
  starting transfers between devices  16.1 us (2%)
  other arithmetic  14.6 us (2%)
    ppermute x26, waiting for transfers between devices, over(): return lax.ppermute(v, axis, perm)  315 us
    pallas_call x5, Pallas kernels, other_part(): pl.pallas_call(functools.partial(other_body, kinds, rows), grid=(tokens /...  206 us
    pallas_call x2, Pallas kernels, logits_part(): pl.pallas_call(functools.partial(logits_body, tile), grid=(count // block...  141 us
    pallas_call x1, Pallas kernels, grads_part(): pl.pallas_call(grads_body, grid_spec=pltpu.PrefetchScalarGridSpec(num_sca...  70.7 us
    pallas_call x6, Pallas kernels, cast_part(): pl.pallas_call(body, grid_spec=pltpu.PrefetchScalarGridSpec(num_scalar_pr...  17.7 us
    pallas_call x4, Pallas kernels, total_part(): pl.pallas_call(body, grid_spec=pltpu.PrefetchScalarGridSpec(num_scalar_pr...  16.6 us
  transfers between devices with their start and end apart: 26, of which 8 were waited for; matrix products, arithmetic and copies ran while one was open for 2% of the time, Pallas kernels for 29%

profile of v2, /device:TPU:0, one launch (start us, length us, event | category | flops | bytes accessed | tf_op | source)
XLA Modules:
  0.0 805.4 jit_solution(10277205584344735418)
XLA Ops:
  0.6 70.6 %logits.2 = (f32[4096,2048]{1,0:T(8,128)}, f32[4096,2048]{1,0:T(8,128)}, f32[8,2048]{1,0:T(8,128)}) custom-call(bf16[4096,3584]{1,0:T(8,128)(2,1)} %ht_ref.13, bf16[4096,1536]{1,0:T(8,128)(2,1)} %hs_ref.15, bf16[3584,2048]{1,0:T(8,128)(2,1)} %refs_0_.11, bf16[1536,2048]{1,0:T(8,128)(2,1)} %refs_1_.7), custom_call_target="tpu_custom_call" | custom-call | flops 42949672960 | bytes 75497472 | tf_op jit(solution)/shard_map/logits/pallas_call | solution.py:88
  71.2 1.5 constant_dynamic-update-slice_fusion.1
  72.7 70.6 %logits.3 = (f32[4096,2048]{1,0:T(8,128)}, f32[4096,2048]{1,0:T(8,128)}, f32[8,2048]{1,0:T(8,128)}) custom-call(bf16[4096,3584]{1,0:T(8,128)(2,1)} %ht_ref.13, bf16[4096,1536]{1,0:T(8,128)(2,1)} %hs_ref.15, bf16[3584,2048]{1,0:T(8,128)(2,1)} %refs_0_.11, bf16[1536,2048]{1,0:T(8,128)(2,1)} %refs_1_.7, ...), custom_call_target="tpu_custom_call", output_to_operand_aliasing={{0}: (4, {}), {1}: (5, {})} | custom-call | flops 42949672960 | bytes 75497472 | tf_op jit(solution)/shard_map/logits/pallas_call | solution.py:88
  143.3 1.5 constant_dynamic-update-slice_fusion
  144.7 3.3 collective-permute-start
  148.1 0.7 pad_add_fusion.at_ref
  148.7 1.9 cast.6
  150.7 3.9 cast.7
  154.5 3.0 cast.8
  157.5 3.0 cast.9
  160.5 0.0 collective-permute-done
  160.5 1.0 broadcast_select_fusion.1
  161.5 0.2 subtract_subtract_fusion
  161.7 1.1 fusion.5
  162.8 0.9 stack.37.coef_ref
  163.7 70.7 %grads.1 = (f32[4096,1536]{1,0:T(8,128)}, f32[1544,1024]{1,0:T(8,128)}, f32[1544,1024]{1,0:T(8,128)}) custom-call(s32[1]{0:T(128)} %bitcast.core_ref.half_ref, bf16[4096,1536]{1,0:T(8,128)(2,1)} %hs_ref.15, bf16[1536,2048]{1,0:T(8,128)(2,1)} %refs_1_.7, f32[4096,2048]{1,0:T(8,128)} %get-tuple-element.19.et_ref, f32[4096,2048]{1,0:T(8,128)} %get-tuple-element.20.es_ref, ...), custom_call_target="tpu_custom_call" | custom-call | flops 51539607552 | bytes 123731968 | tf_op jit(solution)/shard_map/grads/pallas_call | solution.py:138
  234.4 0.0 collective-permute-start.1
  234.5 2.9 cast.11
  237.4 0.1 collective-permute-start.17
  237.4 3.0 cast.10
  240.5 2.0 collective-permute-start.13
  242.4 0.1 collective-permute-start.9
  242.5 127.4 %collective-permute-done.9.rest_2_ = f32[1536,128]{1,0:T(8,128)S(1)} collective-permute-done((f32[1536,128]{1,0:T(8,128)}, f32[1536,128]{1,0:T(8,128)S(1)}, u32[]{:S(2)}, u32[]{:S(2)}) %collective-permute-start.9) | collective-permute-done | bytes 786464 | tf_op jit(solution)/shard_map/ppermute | solution.py:273
  369.9 1.5 collective-permute-start.10
  371.4 0.0 collective-permute-start.11
  371.4 17.6 %collective-permute-done.10.rest_3_ = f32[1536,128]{1,0:T(8,128)S(1)} collective-permute-done((f32[1536,128]{1,0:T(8,128)S(1)}, f32[1536,128]{1,0:T(8,128)S(1)}, u32[]{:S(2)}, u32[]{:S(2)}) %collective-permute-start.10) | collective-permute-done | bytes 786464 | tf_op jit(solution)/shard_map/ppermute | solution.py:273
  389.0 0.5 collective-permute-start.5
  389.5 0.0 collective-permute-done.17.rest_0_
  389.5 1.5 collective-permute-start.18
  391.0 0.0 collective-permute-done.13.rest_0_
  391.0 0.5 collective-permute-start.14
  391.5 0.0 collective-permute-done.11.rest_4_
  391.5 2.3 collective-permute-done.12.rest_5_
  393.8 1.5 collective-permute-start.7
  395.3 53.7 %collective-permute-done.5.rest_0_ = f32[5120,128]{1,0:T(8,128)} collective-permute-done((f32[5120,128]{1,0:T(8,128)}, f32[5120,128]{1,0:T(8,128)}, u32[]{:S(2)}, u32[]{:S(2)}) %collective-permute-start.5) | collective-permute-done | bytes 2621472 | tf_op jit(solution)/shard_map/ppermute | solution.py:273
  449.0 0.4 collective-permute-done.18.rest_1_
  449.4 0.1 collective-permute-start.15
  449.5 53.8 %collective-permute-done.14.rest_1_ = f32[5120,128]{1,0:T(8,128)S(1)} collective-permute-done((f32[5120,128]{1,0:T(8,128)S(1)}, f32[5120,128]{1,0:T(8,128)S(1)}, u32[]{:S(2)}, u32[]{:S(2)}) %collective-permute-start.14) | collective-permute-done | bytes 2621472 | tf_op jit(solution)/shard_map/ppermute | solution.py:273
  503.4 0.5 collective-permute-start.16
  503.9 5.9 slice_add_fusion.1.a_ref
  509.9 4.4 slice_add_fusion.a_ref
  514.2 11.3 %collective-permute-done.7.rest_0_ = f32[3584,256]{1,0:T(8,128)} collective-permute-done((f32[3584,256]{1,0:T(8,128)}, f32[3584,256]{1,0:T(8,128)}, u32[]{:S(2)}, u32[]{:S(2)}) %collective-permute-start.7) | collective-permute-done | bytes 3670048 | tf_op jit(solution)/shard_map/ppermute | solution.py:273
  525.5 0.7 collective-permute-start.3
  526.2 0.0 copy-start.5
  526.3 0.5 collective-permute-start.8
  526.8 1.3 collective-permute-start.24
  528.0 1.0 collective-permute-start.2
  529.0 0.5 copy-done.6
  529.5 0.7 copy-done.7
  530.2 42.6 %other.5.rest_4_ = f32[4096,1536]{1,0:T(8,128)} custom-call(bf16[4096,3584]{1,0:T(8,128)(2,1)} %ht_ref.13, bf16[4096,1536]{1,0:T(8,128)(2,1)} %hs_ref.15, f32[8,4096]{1,0:T(8,128)} %stack.37.coef_ref, f32[5120,128]{1,0:T(8,128)} %collective-permute-done.17.rest_0_, f32[5120,128]{1,0:T(8,128)} %copy-done.2, ...), custom_call_target="tpu_custom_call", output_to_operand_aliasing={{}: (7, {})} | custom-call | flops 27917287424 | bytes 102760448 | tf_op jit(solution)/shard_map/other/pallas_call | solution.py:194
  572.8 42.7 %other.6.rest_6_ = f32[4096,1536]{1,0:T(8,128)} custom-call(bf16[4096,3584]{1,0:T(8,128)(2,1)} %ht_ref.13, bf16[4096,1536]{1,0:T(8,128)(2,1)} %hs_ref.15, f32[8,4096]{1,0:T(8,128)} %stack.37.coef_ref, f32[5120,128]{1,0:T(8,128)} %copy-done.1, f32[5120,128]{1,0:T(8,128)} %copy-done.3, f32[5120,128]{1,0:T(8,128)} %copy-done.5, ...), custom_call_target="tpu_custom_call", output_to_operand_aliasing={{}: (7, {})} | custom-call | flops 27917287424 | bytes 102760448 | tf_op jit(solution)/shard_map/other/pallas_call | solution.py:194
  615.5 0.0 collective-permute-start.4
  615.5 0.5 collective-permute-start.23
  616.0 0.0 collective-permute-start.21
  616.1 0.5 collective-permute-start.25
  616.6 48.7 %collective-permute-done.2.b_ref = f32[776,1024]{1,0:T(8,128)} collective-permute-done((f32[776,1024]{1,0:T(8,128)}, f32[776,1024]{1,0:T(8,128)}, u32[]{:S(2)}, u32[]{:S(2)}) %collective-permute-start.2) | collective-permute-done | bytes 3178528 | tf_op jit(solution)/shard_map/ppermute | solution.py:273
  665.2 42.3 %other.7.rest_2_ = f32[4096,1536]{1,0:T(8,128)} custom-call(bf16[4096,3584]{1,0:T(8,128)(2,1)} %ht_ref.13, bf16[4096,1536]{1,0:T(8,128)(2,1)} %hs_ref.15, f32[8,4096]{1,0:T(8,128)} %stack.37.coef_ref, f32[3584,256]{1,0:T(8,128)} %collective-permute-done.7.rest_0_, f32[3584,256]{1,0:T(8,128)} %collective-permute-done.8.rest_1_, ...), custom_call_target="tpu_custom_call", output_to_operand_aliasing={{}: (9, {})} | custom-call | flops 27917287424 | bytes 102760448 | tf_op jit(solution)/shard_map/other/pallas_call | solution.py:194
  707.6 39.1 %other.8.rest_2_ = f32[4096,1536]{1,0:T(8,128)} custom-call(bf16[4096,3584]{1,0:T(8,128)(2,1)} %ht_ref.13, bf16[4096,1536]{1,0:T(8,128)(2,1)} %hs_ref.15, f32[8,4096]{1,0:T(8,128)} %stack.37.coef_ref, f32[5120,128]{1,0:T(8,128)} %collective-permute-done.5.rest_0_, f32[5120,128]{1,0:T(8,128)} %collective-permute-done.6.rest_1_, ...), custom_call_target="tpu_custom_call", output_to_operand_aliasing={{}: (5, {})} | custom-call | flops 13958643712 | bytes 97517568 | tf_op jit(solution)/shard_map/other/pallas_call | solution.py:194
  746.7 38.9 %other.9 = f32[4096,1536]{1,0:T(8,128)} custom-call(bf16[4096,3584]{1,0:T(8,128)(2,1)} %ht_ref.13, bf16[4096,1536]{1,0:T(8,128)(2,1)} %hs_ref.15, f32[8,4096]{1,0:T(8,128)} %stack.37.coef_ref, f32[5120,128]{1,0:T(8,128)} %collective-permute-done.3.rest_0_, f32[5120,128]{1,0:T(8,128)} %collective-permute-done.4.rest_1_, ...), custom_call_target="tpu_custom_call", output_to_operand_aliasing={{}: (5, {})} | custom-call | flops 13958643712 | bytes 97517568 | tf_op jit(solution)/shard_map/other/pallas_call | solution.py:194
  785.6 4.1 total.4.rest_0_
  789.7 1.4 fusion.8
  791.8 4.2 total.5.rest_0_
  795.9 4.1 total.6.rest_0_
  800.1 4.2 total.7
  (41 shorter events, 0.1 us)
Async XLA Ops:
  144.7 15.8 %collective-permute-start = (f32[8,4096]{1,0:T(8,128)}, f32[8,4096]{1,0:T(8,128)}, u32[]{:S(2)}, u32[]{:S(2)}) collective-permute-start(f32[8,4096]{1,0:T(8,128)} %constant_dynamic-update-slice_fusion), channel_id=1, source_target_pairs={{0,4},{4,0},{1,5},{5,1},{2,6},{6,2},{3,7},{7,3}} | collective-permute-start | bytes 393224 | tf_op jit(solution)/shard_map/ppermute | solution.py:273
  234.4 269.0 %collective-permute-start.1 = (f32[1544,1024]{1,0:T(8,128)}, f32[1544,1024]{1,0:T(8,128)}, u32[]{:S(2)}, u32[]{:S(2)}) collective-permute-start(f32[1544,1024]{1,0:T(8,128)} %get-tuple-element.25), channel_id=1, source_target_pairs={{0,1},{1,0},{2,3},{3,2},{4,5},{5,4},{6,7},{7,6}} | collective-permute-start | bytes 18972680 | tf_op jit(solution)/shard_map/ppermute | solution.py:273
  237.4 152.1 %collective-permute-start.17 = (f32[5120,128]{1,0:T(8,128)}, f32[5120,128]{1,0:T(8,128)}, u32[]{:S(2)}, u32[]{:S(2)}) collective-permute-start(f32[5120,128]{1,0:T(8,128)} %cast.11), channel_id=1, source_target_pairs={{0,4},{4,0},{1,5},{5,1},{2,6},{6,2},{3,7},{7,3}} | collective-permute-start | bytes 7864328 | tf_op jit(solution)/shard_map/ppermute | solution.py:273
  240.5 150.5 %collective-permute-start.13 = (f32[5120,128]{1,0:T(8,128)}, f32[5120,128]{1,0:T(8,128)S(1)}, u32[]{:S(2)}, u32[]{:S(2)}) collective-permute-start(f32[5120,128]{1,0:T(8,128)} %cast.10), channel_id=1, source_target_pairs={{0,4},{4,0},{1,5},{5,1},{2,6},{6,2},{3,7},{7,3}} | collective-permute-start | bytes 7864328 | tf_op jit(solution)/shard_map/ppermute | solution.py:273
  242.4 127.5 %collective-permute-start.9 = (f32[1536,128]{1,0:T(8,128)}, f32[1536,128]{1,0:T(8,128)S(1)}, u32[]{:S(2)}, u32[]{:S(2)}) collective-permute-start(f32[1536,128]{1,0:T(8,128)} %cast.6), channel_id=1, source_target_pairs={{0,4},{4,0},{1,5},{5,1},{2,6},{6,2},{3,7},{7,3}} | collective-permute-start | bytes 2359304 | tf_op jit(solution)/shard_map/ppermute | solution.py:273
  369.9 133.5 %copy-start.8 = (f32[1536,128]{1,0:T(8,128)}, f32[1536,128]{1,0:T(8,128)S(1)}, u32[]{:S(2)}) copy-start(f32[1536,128]{1,0:T(8,128)S(1)} %collective-permute-done.9.rest_2_) | copy-start | bytes 2359300
  369.9 19.1 %collective-permute-start.10 = (f32[1536,128]{1,0:T(8,128)S(1)}, f32[1536,128]{1,0:T(8,128)S(1)}, u32[]{:S(2)}, u32[]{:S(2)}) collective-permute-start(f32[1536,128]{1,0:T(8,128)S(1)} %collective-permute-done.9.rest_2_), channel_id=1, source_target_pairs={{0,2},{1,3},{2,0},{3,1},{4,6},{5,7},{6,4},{7,5}} | collective-permute-start | bytes 2359304 | tf_op jit(solution)/shard_map/ppermute | solution.py:273
  371.4 20.2 %collective-permute-start.11 = (f32[1536,128]{1,0:T(8,128)S(1)}, f32[1536,128]{1,0:T(8,128)S(1)}, u32[]{:S(2)}, u32[]{:S(2)}) collective-permute-start(f32[1536,128]{1,0:T(8,128)S(1)} %collective-permute-done.9.rest_2_), channel_id=1, source_target_pairs={{0,1},{1,0},{2,3},{3,2},{4,5},{5,4},{6,7},{7,6}} | collective-permute-start | bytes 2359304 | tf_op jit(solution)/shard_map/ppermute | solution.py:273
  389.0 114.4 %copy-start.9 = (f32[1536,128]{1,0:T(8,128)}, f32[1536,128]{1,0:T(8,128)S(1)}, u32[]{:S(2)}) copy-start(f32[1536,128]{1,0:T(8,128)S(1)} %collective-permute-done.10.rest_3_) | copy-start | bytes 2359300
  389.0 60.1 %collective-permute-start.5 = (f32[5120,128]{1,0:T(8,128)}, f32[5120,128]{1,0:T(8,128)}, u32[]{:S(2)}, u32[]{:S(2)}) collective-permute-start(f32[5120,128]{1,0:T(8,128)} %cast.8), channel_id=1, source_target_pairs={{0,4},{4,0},{1,5},{5,1},{2,6},{6,2},{3,7},{7,3}} | collective-permute-start | bytes 7864328 | tf_op jit(solution)/shard_map/ppermute | solution.py:273
  389.5 59.9 %collective-permute-start.18 = (f32[5120,128]{1,0:T(8,128)}, f32[5120,128]{1,0:T(8,128)S(1)}, u32[]{:S(2)}, u32[]{:S(2)}) collective-permute-start(f32[5120,128]{1,0:T(8,128)} %collective-permute-done.17.rest_0_), channel_id=1, source_target_pairs={{0,2},{1,3},{2,0},{3,1},{4,6},{5,7},{6,4},{7,5}} | collective-permute-start | bytes 7864328 | tf_op jit(solution)/shard_map/ppermute | solution.py:273
  391.0 118.9 %copy-start.1 = (f32[5120,128]{1,0:T(8,128)}, f32[5120,128]{1,0:T(8,128)S(1)}, u32[]{:S(2)}) copy-start(f32[5120,128]{1,0:T(8,128)S(1)} %collective-permute-done.13.rest_0_) | copy-start | bytes 7864324
  391.0 112.4 %collective-permute-start.14 = (f32[5120,128]{1,0:T(8,128)S(1)}, f32[5120,128]{1,0:T(8,128)S(1)}, u32[]{:S(2)}, u32[]{:S(2)}) collective-permute-start(f32[5120,128]{1,0:T(8,128)S(1)} %collective-permute-done.13.rest_0_), channel_id=1, source_target_pairs={{0,2},{1,3},{2,0},{3,1},{4,6},{5,7},{6,4},{7,5}} | collective-permute-start | bytes 7864328 | tf_op jit(solution)/shard_map/ppermute | solution.py:273
  391.5 111.9 %copy-start.10 = (f32[1536,128]{1,0:T(8,128)}, f32[1536,128]{1,0:T(8,128)S(1)}, u32[]{:S(2)}) copy-start(f32[1536,128]{1,0:T(8,128)S(1)} %collective-permute-done.11.rest_4_) | copy-start | bytes 2359300
  391.5 2.3 collective-permute-start.12
  393.8 109.6 %copy-start.11 = (f32[1536,128]{1,0:T(8,128)}, f32[1536,128]{1,0:T(8,128)S(1)}, u32[]{:S(2)}) copy-start(f32[1536,128]{1,0:T(8,128)S(1)} %collective-permute-done.12.rest_5_) | copy-start | bytes 2359300
  393.8 131.7 %collective-permute-start.7 = (f32[3584,256]{1,0:T(8,128)}, f32[3584,256]{1,0:T(8,128)}, u32[]{:S(2)}, u32[]{:S(2)}) collective-permute-start(f32[3584,256]{1,0:T(8,128)} %cast.7), channel_id=1, source_target_pairs={{0,4},{4,0},{1,5},{5,1},{2,6},{6,2},{3,7},{7,3}} | collective-permute-start | bytes 11010056 | tf_op jit(solution)/shard_map/ppermute | solution.py:273
  449.0 77.2 %collective-permute-start.19 = (f32[5120,128]{1,0:T(8,128)}, f32[5120,128]{1,0:T(8,128)S(1)}, u32[]{:S(2)}, u32[]{:S(2)}) collective-permute-start(f32[5120,128]{1,0:T(8,128)} %collective-permute-done.17.rest_0_), channel_id=1, source_target_pairs={{0,1},{1,0},{2,3},{3,2},{4,5},{5,4},{6,7},{7,6}} | collective-permute-start | bytes 7864328 | tf_op jit(solution)/shard_map/ppermute | solution.py:273
  449.4 60.4 %copy-start.2 = (f32[5120,128]{1,0:T(8,128)}, f32[5120,128]{1,0:T(8,128)S(1)}, u32[]{:S(2)}) copy-start(f32[5120,128]{1,0:T(8,128)S(1)} %collective-permute-done.18.rest_1_) | copy-start | bytes 7864324
  449.4 76.8 %collective-permute-start.15 = (f32[5120,128]{1,0:T(8,128)S(1)}, f32[5120,128]{1,0:T(8,128)S(1)}, u32[]{:S(2)}, u32[]{:S(2)}) collective-permute-start(f32[5120,128]{1,0:T(8,128)S(1)} %collective-permute-done.13.rest_0_), channel_id=1, source_target_pairs={{0,1},{1,0},{2,3},{3,2},{4,5},{5,4},{6,7},{7,6}} | collective-permute-start | bytes 7864328 | tf_op jit(solution)/shard_map/ppermute | solution.py:273
  503.4 6.5 copy-start.3
  503.4 23.4 %collective-permute-start.20 = (f32[5120,128]{1,0:T(8,128)S(1)}, f32[5120,128]{1,0:T(8,128)S(1)}, u32[]{:S(2)}, u32[]{:S(2)}) collective-permute-start(f32[5120,128]{1,0:T(8,128)S(1)} %collective-permute-done.18.rest_1_), channel_id=1, source_target_pairs={{0,1},{1,0},{2,3},{3,2},{4,5},{5,4},{6,7},{7,6}} | collective-permute-start | bytes 7864328 | tf_op jit(solution)/shard_map/ppermute | solution.py:273
  503.4 24.6 %collective-permute-start.16 = (f32[5120,128]{1,0:T(8,128)S(1)}, f32[5120,128]{1,0:T(8,128)S(1)}, u32[]{:S(2)}, u32[]{:S(2)}) collective-permute-start(f32[5120,128]{1,0:T(8,128)S(1)} %collective-permute-done.14.rest_1_), channel_id=1, source_target_pairs={{0,1},{1,0},{2,3},{3,2},{4,5},{5,4},{6,7},{7,6}} | collective-permute-start | bytes 7864328 | tf_op jit(solution)/shard_map/ppermute | solution.py:273
  503.9 5.9 copy-start
  525.5 90.0 %collective-permute-start.3 = (f32[5120,128]{1,0:T(8,128)}, f32[5120,128]{1,0:T(8,128)}, u32[]{:S(2)}, u32[]{:S(2)}) collective-permute-start(f32[5120,128]{1,0:T(8,128)} %cast.9), channel_id=1, source_target_pairs={{0,4},{4,0},{1,5},{5,1},{2,6},{6,2},{3,7},{7,3}} | collective-permute-start | bytes 7864328 | tf_op jit(solution)/shard_map/ppermute | solution.py:273
  526.2 1.8 copy-start.4
  526.2 89.3 %collective-permute-start.6 = (f32[5120,128]{1,0:T(8,128)}, f32[5120,128]{1,0:T(8,128)}, u32[]{:S(2)}, u32[]{:S(2)}) collective-permute-start(f32[5120,128]{1,0:T(8,128)} %collective-permute-done.5.rest_0_), channel_id=1, source_target_pairs={{0,1},{1,0},{2,3},{3,2},{4,5},{5,4},{6,7},{7,6}} | collective-permute-start | bytes 7864328 | tf_op jit(solution)/shard_map/ppermute | solution.py:273
  526.2 2.8 copy-start.5
  526.3 89.8 %collective-permute-start.8 = (f32[3584,256]{1,0:T(8,128)}, f32[3584,256]{1,0:T(8,128)}, u32[]{:S(2)}, u32[]{:S(2)}) collective-permute-start(f32[3584,256]{1,0:T(8,128)} %collective-permute-done.7.rest_0_), channel_id=1, source_target_pairs={{0,1},{1,0},{2,3},{3,2},{4,5},{5,4},{6,7},{7,6}} | collective-permute-start | bytes 11010056 | tf_op jit(solution)/shard_map/ppermute | solution.py:273
  526.8 2.7 copy-start.6
  526.8 89.3 %collective-permute-start.24 = (f32[768,1024]{1,0:T(8,128)}, f32[768,1024]{1,0:T(8,128)}, u32[]{:S(2)}, u32[]{:S(2)}) collective-permute-start(f32[768,1024]{1,0:T(8,128)} %slice_add_fusion.1.a_ref), channel_id=1, source_target_pairs={{0,2},{1,3},{2,0},{3,1},{4,6},{5,7},{6,4},{7,5}} | collective-permute-start | bytes 9437192 | tf_op jit(solution)/shard_map/ppermute | solution.py:273
  528.0 2.2 copy-start.7
  528.0 137.2 %collective-permute-start.2 = (f32[776,1024]{1,0:T(8,128)}, f32[776,1024]{1,0:T(8,128)}, u32[]{:S(2)}, u32[]{:S(2)}) collective-permute-start(f32[776,1024]{1,0:T(8,128)} %slice_add_fusion.a_ref), channel_id=1, source_target_pairs={{0,2},{1,3},{2,0},{3,1},{4,6},{5,7},{6,4},{7,5}} | collective-permute-start | bytes 9535496 | tf_op jit(solution)/shard_map/ppermute | solution.py:273
  615.5 131.2 %collective-permute-start.4 = (f32[5120,128]{1,0:T(8,128)}, f32[5120,128]{1,0:T(8,128)}, u32[]{:S(2)}, u32[]{:S(2)}) collective-permute-start(f32[5120,128]{1,0:T(8,128)} %collective-permute-done.3.rest_0_), channel_id=1, source_target_pairs={{0,1},{1,0},{2,3},{3,2},{4,5},{5,4},{6,7},{7,6}} | collective-permute-start | bytes 7864328 | tf_op jit(solution)/shard_map/ppermute | solution.py:273
  615.5 176.2 %collective-permute-start.23 = (f32[768,1024]{1,0:T(8,128)}, f32[768,1024]{1,0:T(8,128)}, u32[]{:S(2)}, u32[]{:S(2)}) collective-permute-start(f32[768,1024]{1,0:T(8,128)} %slice_add_fusion.1.a_ref), channel_id=1, source_target_pairs={{0,1},{1,0},{2,3},{3,2},{4,5},{5,4},{6,7},{7,6}} | collective-permute-start | bytes 9437192 | tf_op jit(solution)/shard_map/ppermute | solution.py:273
  616.0 184.0 %collective-permute-start.21 = (f32[776,1024]{1,0:T(8,128)}, f32[776,1024]{1,0:T(8,128)}, u32[]{:S(2)}, u32[]{:S(2)}) collective-permute-start(f32[776,1024]{1,0:T(8,128)} %slice_add_fusion.a_ref), channel_id=1, source_target_pairs={{0,1},{1,0},{2,3},{3,2},{4,5},{5,4},{6,7},{7,6}} | collective-permute-start | bytes 9535496 | tf_op jit(solution)/shard_map/ppermute | solution.py:273
  616.1 175.7 %collective-permute-start.25 = (f32[768,1024]{1,0:T(8,128)}, f32[768,1024]{1,0:T(8,128)}, u32[]{:S(2)}, u32[]{:S(2)}) collective-permute-start(f32[768,1024]{1,0:T(8,128)} %collective-permute-done.24.b_ref), channel_id=1, source_target_pairs={{0,1},{1,0},{2,3},{3,2},{4,5},{5,4},{6,7},{7,6}} | collective-permute-start | bytes 9437192 | tf_op jit(solution)/shard_map/ppermute | solution.py:273
  665.2 134.8 %collective-permute-start.22 = (f32[776,1024]{1,0:T(8,128)}, f32[776,1024]{1,0:T(8,128)}, u32[]{:S(2)}, u32[]{:S(2)}) collective-permute-start(f32[776,1024]{1,0:T(8,128)} %collective-permute-done.2.b_ref), channel_id=1, source_target_pairs={{0,1},{1,0},{2,3},{3,2},{4,5},{5,4},{6,7},{7,6}} | collective-permute-start | bytes 9535496 | tf_op jit(solution)/shard_map/ppermute | solution.py:273

commit v3 on v2

--- a/solution.py
+++ b/solution.py
@@ -28,49 +28,49 @@
     return acc
 
 
-def logits_body(tile, ht_ref, hs_ref, wt_ref, ws_ref, *rest):
+def logits_body(rows, tile, ht_ref, hs_ref, wt_ref, ws_ref, *rest):
     et_ref, es_ref, stat_ref = rest[-3:]
-    rows, cols = et_ref.shape
-    low = jnp.full((rows, 128), -jnp.inf, F32)
-
-    def products(c, carry):
-        mt, ms = carry
-        at = pl.ds(pl.multiple_of(c * tile, tile), tile)
-        zt = jnp.dot(ht_ref[...], wt_ref[:, at], preferred_element_type=F32)
-        et_ref[:, at] = zt
-        mt = jnp.maximum(mt, lane_fold(zt, jnp.maximum))
-        zs = jnp.dot(hs_ref[...], ws_ref[:, at], preferred_element_type=F32)
-        es_ref[:, at] = zs
-        return mt, jnp.maximum(ms, lane_fold(zs, jnp.maximum))
-
-    mt, ms = lax.fori_loop(0, cols // tile, products, (low, low))
-    mt = jnp.max(mt, axis=1, keepdims=True)
-    ms = jnp.max(ms, axis=1, keepdims=True)
-    zero = jnp.zeros((rows, 128), F32)
-    step = 256
-
-    def exps(c, carry):
-        st, ss, dd = carry
-        at = pl.ds(pl.multiple_of(c * step, step), step)
-        xt = et_ref[:, at] - mt
-        xs = es_ref[:, at] - ms
-        pt = jnp.exp(xt)
-        ps = jnp.exp(xs)
-        et_ref[:, at] = pt
-        es_ref[:, at] = ps
-        return st + lane_fold(pt, jnp.add), ss + lane_fold(ps, jnp.add), dd + lane_fold(pt * (xt - xs), jnp.add)
-
-    st, ss, dd = lax.fori_loop(0, cols // step, exps, (zero, zero, zero))
-    vals = (mt, jnp.sum(st, axis=1, keepdims=True), ms, jnp.sum(ss, axis=1, keepdims=True),
-            jnp.sum(dd, axis=1, keepdims=True))
-    lane = lax.broadcasted_iota(jnp.int32, (rows, 128), 1)
-    packed = zero
-    for i, v in enumerate(vals):
-        packed = jnp.where(lane == i, v, packed)
-    stat_ref[...] = jnp.transpose(packed)[0:8, :]
-
-
-def logits_part(ht, hs, wt, ws, start, count, prev, block=512, tile=512):
+    block, cols = et_ref.shape
+
+    @pl.loop(0, block, step=rows)
+    def _(r):
+        sl = pl.ds(pl.multiple_of(r, rows), rows)
+        ht = ht_ref[sl, :]
+        hs = hs_ref[sl, :]
+        mt = jnp.full((rows, 128), -jnp.inf, F32)
+        ms = mt
+        for c in range(0, cols, tile):
+            zt = jnp.dot(ht, wt_ref[:, c:c + tile], preferred_element_type=F32)
+            et_ref[sl, c:c + tile] = zt
+            mt = jnp.maximum(mt, lane_fold(zt, jnp.maximum))
+            zs = jnp.dot(hs, ws_ref[:, c:c + tile], preferred_element_type=F32)
+            es_ref[sl, c:c + tile] = zs
+            ms = jnp.maximum(ms, lane_fold(zs, jnp.maximum))
+        mt = jnp.max(mt, axis=1, keepdims=True)
+        ms = jnp.max(ms, axis=1, keepdims=True)
+        st = jnp.zeros((rows, 128), F32)
+        ss = st
+        dd = st
+        for c in range(0, cols, 128):
+            xt = et_ref[sl, c:c + 128] - mt
+            xs = es_ref[sl, c:c + 128] - ms
+            pt = jnp.exp(xt)
+            ps = jnp.exp(xs)
+            et_ref[sl, c:c + 128] = pt
+            es_ref[sl, c:c + 128] = ps
+            st = st + pt
+            ss = ss + ps
+            dd = dd + pt * (xt - xs)
+        vals = (mt, jnp.sum(st, axis=1, keepdims=True), ms, jnp.sum(ss, axis=1, keepdims=True),
+                jnp.sum(dd, axis=1, keepdims=True))
+        lane = lax.broadcasted_iota(jnp.int32, (rows, 128), 1)
+        packed = jnp.zeros((rows, 128), F32)
+        for i, v in enumerate(vals):
+            packed = jnp.where(lane == i, v, packed)
+        stat_ref[:, sl] = jnp.transpose(packed)[0:8, :]
+
+
+def logits_part(ht, hs, wt, ws, start, count, prev, block=512, rows=256, tile=512):
     tokens, kt = ht.shape
     ks, cols = ws.shape
     first = start // block
@@ -86,7 +86,7 @@
         args += list(prev)
         alias = {4: 0, 5: 1}
     return pl.pallas_call(
-        functools.partial(logits_body, tile),
+        functools.partial(logits_body, rows, tile),
         grid=(count // block,),
         in_specs=in_specs,
         out_specs=[pl.BlockSpec((block, cols), tok), pl.BlockSpec((block, cols), tok),
@@ -329,11 +329,10 @@
         beside_a, beside_b = to_core(chip_a), to_core(chip_b)
         cross_a, cross_b = to_core(far_a), to_core(far_b)
 
-        for pieces in ((("ts", y0), ("ts", x0), ("ts", cy0), ("ts", cx0)),
-                             (("ts", y1), ("ts", x1), ("ts", cy1), ("ts", cx1)),
+        for pieces in ((("ts", y0), ("ts", x0), ("ts", cy0), ("ts", cx0),
+                                     ("ts", y1), ("ts", x1), ("ts", cy1), ("ts", cx1)),
                              (("t", y2t), ("t", cy2t), ("s", y2s), ("s", x2s), ("s", cy2s), ("s", cx2s)),
-                             (("ts", y3), ("ts", cy3)),
-                             (("ts", y4), ("ts", cy4))):
+                             (("ts", y3), ("ts", cy3), ("ts", y4), ("ts", cy4))):
             dh = other_part(h_teacher, h_student, coef, pieces, dh)
 
         shape = w_student.shape

time: 806 us -> 788 us (0.978)
  Pallas kernels: 452 us -> 391 us
  waiting for transfers between devices: 315 us -> 357 us
    pallas_call x5 -> x3, Pallas kernels: 206 us -> 160 us  [other_part(): pl.pallas_call(functools.partial(other_body, kinds, rows), grid=(tokens /...]
    ppermute x26, waiting for transfers between devices: 315 us -> 357 us  [over(): return lax.ppermute(v, axis, perm)]
    pallas_call x2, Pallas kernels: 141 us -> 126 us  [logits_part(): pl.pallas_call(functools.partial(logits_body, rows, tile), grid=(count //...]
  transfers between devices with their start and end apart: 26 -> 26, of which waited for: 8 -> 9; matrix products, arithmetic and copies ran while one was open for 2% -> 2% of each run, Pallas kernels for 29% -> 24%
where the time goes in v3:
time: 788 us
  Pallas kernels  391 us (50%)
  waiting for transfers between devices  357 us (45%)
  starting transfers between devices  17 us (2%)
  other arithmetic  15 us (2%)
    ppermute x26, waiting for transfers between devices, over(): return lax.ppermute(v, axis, perm)  357 us
    pallas_call x3, Pallas kernels, other_part(): pl.pallas_call(functools.partial(other_body, kinds, rows), grid=(tokens /...  160 us
    pallas_call x2, Pallas kernels, logits_part(): pl.pallas_call(functools.partial(logits_body, rows, tile), grid=(count //...  126 us
    pallas_call x1, Pallas kernels, grads_part(): pl.pallas_call(grads_body, grid_spec=pltpu.PrefetchScalarGridSpec(num_sca...  70.7 us
    pallas_call x6, Pallas kernels, cast_part(): pl.pallas_call(body, grid_spec=pltpu.PrefetchScalarGridSpec(num_scalar_pr...  17.7 us
    ppermute x26, starting transfers between devices, over(): return lax.ppermute(v, axis, perm)  17 us
    pallas_call x4, Pallas kernels, total_part(): pl.pallas_call(body, grid_spec=pltpu.PrefetchScalarGridSpec(num_scalar_pr...  16.6 us
  transfers between devices with their start and end apart: 26, of which 9 were waited for; matrix products, arithmetic and copies ran while one was open for 2% of the time, Pallas kernels for 24%

profile of v3, /device:TPU:0, one launch (start us, length us, event | category | flops | bytes accessed | tf_op | source)
XLA Modules:
  0.0 787.7 jit_solution(10759786287299763148)
XLA Ops:
  0.6 62.9 %logits.2 = (f32[4096,2048]{1,0:T(8,128)}, f32[4096,2048]{1,0:T(8,128)}, f32[8,2048]{1,0:T(8,128)}) custom-call(bf16[4096,3584]{1,0:T(8,128)(2,1)} %ht_ref.9, bf16[4096,1536]{1,0:T(8,128)(2,1)} %hs_ref.11, bf16[3584,2048]{1,0:T(8,128)(2,1)} %refs_0_.11, bf16[1536,2048]{1,0:T(8,128)(2,1)} %refs_1_.7), custom_call_target="tpu_custom_call" | custom-call | flops 42949672960 | bytes 75497472 | tf_op jit(solution)/shard_map/logits/pallas_call | solution.py:88
  63.6 1.5 constant_dynamic-update-slice_fusion.1
  65.0 62.9 %logits.3 = (f32[4096,2048]{1,0:T(8,128)}, f32[4096,2048]{1,0:T(8,128)}, f32[8,2048]{1,0:T(8,128)}) custom-call(bf16[4096,3584]{1,0:T(8,128)(2,1)} %ht_ref.9, bf16[4096,1536]{1,0:T(8,128)(2,1)} %hs_ref.11, bf16[3584,2048]{1,0:T(8,128)(2,1)} %refs_0_.11, bf16[1536,2048]{1,0:T(8,128)(2,1)} %refs_1_.7, ...), custom_call_target="tpu_custom_call", output_to_operand_aliasing={{0}: (4, {}), {1}: (5, {})} | custom-call | flops 42949672960 | bytes 75497472 | tf_op jit(solution)/shard_map/logits/pallas_call | solution.py:88
  128.0 1.5 constant_dynamic-update-slice_fusion
  129.4 3.3 collective-permute-start
  132.8 0.7 pad_add_fusion.at_ref
  133.4 1.9 cast.6
  135.4 3.9 cast.7
  139.2 3.0 cast.8
  142.2 3.0 cast.9
  145.2 0.0 collective-permute-done
  145.2 1.0 broadcast_select_fusion.1
  146.2 0.2 subtract_subtract_fusion
  146.4 1.1 fusion.5
  147.5 0.9 stack.37.coef_ref
  148.4 70.7 %grads.1 = (f32[4096,1536]{1,0:T(8,128)}, f32[1544,1024]{1,0:T(8,128)}, f32[1544,1024]{1,0:T(8,128)}) custom-call(s32[1]{0:T(128)} %bitcast.core_ref.half_ref, bf16[4096,1536]{1,0:T(8,128)(2,1)} %hs_ref.11, bf16[1536,2048]{1,0:T(8,128)(2,1)} %refs_1_.7, f32[4096,2048]{1,0:T(8,128)} %get-tuple-element.19.et_ref, f32[4096,2048]{1,0:T(8,128)} %get-tuple-element.20.es_ref, ...), custom_call_target="tpu_custom_call" | custom-call | flops 51539607552 | bytes 123731968 | tf_op jit(solution)/shard_map/grads/pallas_call | solution.py:138
  219.1 0.0 collective-permute-start.1
  219.2 0.0 collective-permute-start.9
  219.2 2.9 cast.11
  222.1 2.0 collective-permute-start.17
  224.1 3.0 cast.10
  227.2 0.0 collective-permute-start.13
  227.2 12.7 %collective-permute-done.9.rest_2_ = f32[1536,128]{1,0:T(8,128)} collective-permute-done((f32[1536,128]{1,0:T(8,128)}, f32[1536,128]{1,0:T(8,128)}, u32[]{:S(2)}, u32[]{:S(2)}) %collective-permute-start.9) | collective-permute-done | bytes 786464 | tf_op jit(solution)/shard_map/ppermute | solution.py:273
  239.9 1.5 collective-permute-start.10
  241.4 0.0 collective-permute-start.11
  241.4 17.3 %collective-permute-done.10.rest_3_ = f32[1536,128]{1,0:T(8,128)S(1)} collective-permute-done((f32[1536,128]{1,0:T(8,128)}, f32[1536,128]{1,0:T(8,128)S(1)}, u32[]{:S(2)}, u32[]{:S(2)}) %collective-permute-start.10) | collective-permute-done | bytes 786464 | tf_op jit(solution)/shard_map/ppermute | solution.py:273
  258.7 0.5 collective-permute-start.3
  259.2 0.0 collective-permute-done.11.rest_4_
  259.3 2.3 collective-permute-done.12.rest_5_
  261.5 1.5 collective-permute-start.5
  263.0 33.1 %collective-permute-done.17.rest_4_ = f32[5120,128]{1,0:T(8,128)} collective-permute-done((f32[5120,128]{1,0:T(8,128)}, f32[5120,128]{1,0:T(8,128)}, u32[]{:S(2)}, u32[]{:S(2)}) %collective-permute-start.17) | collective-permute-done | bytes 2621472 | tf_op jit(solution)/shard_map/ppermute | solution.py:273
  296.1 1.5 collective-permute-start.18
  297.6 54.6 %collective-permute-done.13.rest_0_ = f32[5120,128]{1,0:T(8,128)S(1)} collective-permute-done((f32[5120,128]{1,0:T(8,128)}, f32[5120,128]{1,0:T(8,128)S(1)}, u32[]{:S(2)}, u32[]{:S(2)}) %collective-permute-start.13) | collective-permute-done | bytes 2621472 | tf_op jit(solution)/shard_map/ppermute | solution.py:273
  352.2 1.5 collective-permute-start.14
  353.7 54.8 %collective-permute-done.3.rest_0_ = f32[5120,128]{1,0:T(8,128)} collective-permute-done((f32[5120,128]{1,0:T(8,128)}, f32[5120,128]{1,0:T(8,128)}, u32[]{:S(2)}, u32[]{:S(2)}) %collective-permute-start.3) | collective-permute-done | bytes 2621472 | tf_op jit(solution)/shard_map/ppermute | solution.py:273
  408.4 0.0 collective-permute-start.7
  408.5 56.2 %collective-permute-done.5.rest_2_ = f32[5120,128]{1,0:T(8,128)} collective-permute-done((f32[5120,128]{1,0:T(8,128)}, f32[5120,128]{1,0:T(8,128)}, u32[]{:S(2)}, u32[]{:S(2)}) %collective-permute-start.5) | collective-permute-done | bytes 2621472 | tf_op jit(solution)/shard_map/ppermute | solution.py:273
  464.6 0.0 collective-permute-start.19
  464.6 0.0 collective-permute-done.18.rest_5_
  464.6 0.5 collective-permute-start.15
  465.1 0.0 collective-permute-done.14.rest_1_
  465.1 0.0 collective-permute-start.20
  465.2 0.5 collective-permute-start.16
  465.7 6.3 slice_add_fusion.1.a_ref
  472.0 4.4 slice_add_fusion.a_ref
  476.4 66.4 %collective-permute-done.7.rest_0_ = f32[3584,256]{1,0:T(8,128)} collective-permute-done((f32[3584,256]{1,0:T(8,128)}, f32[3584,256]{1,0:T(8,128)}, u32[]{:S(2)}, u32[]{:S(2)}) %collective-permute-start.7) | collective-permute-done | bytes 3670048 | tf_op jit(solution)/shard_map/ppermute | solution.py:273
  542.8 0.5 collective-permute-start.6
  543.3 0.0 collective-permute-start.8
  543.4 1.5 collective-permute-start.24
  544.8 0.9 collective-permute-start.2
  545.7 0.3 copy-done.6
  546.0 0.7 copy-done.7
  546.8 74.6 %other.3.rest_6_ = f32[4096,1536]{1,0:T(8,128)} custom-call(bf16[4096,3584]{1,0:T(8,128)(2,1)} %ht_ref.9, bf16[4096,1536]{1,0:T(8,128)(2,1)} %hs_ref.11, f32[8,4096]{1,0:T(8,128)} %stack.37.coef_ref, f32[5120,128]{1,0:T(8,128)} %copy-done.1, f32[5120,128]{1,0:T(8,128)} %copy-done.3, f32[5120,128]{1,0:T(8,128)} %copy-done.5, ...), custom_call_target="tpu_custom_call", output_to_operand_aliasing={{}: (11, {})} | custom-call | flops 55834574848 | bytes 113246208 | tf_op jit(solution)/shard_map/other/pallas_call | solution.py:194
  621.3 0.5 collective-permute-start.23
  621.9 0.0 collective-permute-start.21
  621.9 0.5 collective-permute-start.25
  622.4 59.9 %collective-permute-done.2.b_ref = f32[776,1024]{1,0:T(8,128)} collective-permute-done((f32[776,1024]{1,0:T(8,128)}, f32[776,1024]{1,0:T(8,128)}, u32[]{:S(2)}, u32[]{:S(2)}) %collective-permute-start.2) | collective-permute-done | bytes 3178528 | tf_op jit(solution)/shard_map/ppermute | solution.py:273
  682.3 42.6 %other.4.rest_4_ = f32[4096,1536]{1,0:T(8,128)} custom-call(bf16[4096,3584]{1,0:T(8,128)(2,1)} %ht_ref.9, bf16[4096,1536]{1,0:T(8,128)(2,1)} %hs_ref.11, f32[8,4096]{1,0:T(8,128)} %stack.37.coef_ref, f32[3584,256]{1,0:T(8,128)} %collective-permute-done.7.rest_0_, f32[3584,256]{1,0:T(8,128)} %collective-permute-done.8.rest_1_, ...), custom_call_target="tpu_custom_call", output_to_operand_aliasing={{}: (9, {})} | custom-call | flops 27917287424 | bytes 102760448 | tf_op jit(solution)/shard_map/other/pallas_call | solution.py:194
  724.9 42.9 %other.5 = f32[4096,1536]{1,0:T(8,128)} custom-call(bf16[4096,3584]{1,0:T(8,128)(2,1)} %ht_ref.9, bf16[4096,1536]{1,0:T(8,128)(2,1)} %hs_ref.11, f32[8,4096]{1,0:T(8,128)} %stack.37.coef_ref, f32[5120,128]{1,0:T(8,128)} %collective-permute-done.3.rest_0_, f32[5120,128]{1,0:T(8,128)} %collective-permute-done.4.rest_1_, ...), custom_call_target="tpu_custom_call", output_to_operand_aliasing={{}: (7, {})} | custom-call | flops 27917287424 | bytes 102760448 | tf_op jit(solution)/shard_map/other/pallas_call | solution.py:194
  767.8 4.1 total.4.rest_0_
  772.0 1.4 fusion.8
  774.0 4.2 total.5.rest_0_
  778.2 4.1 total.6.rest_0_
  782.4 4.2 total.7
  (37 shorter events, 0.1 us)
Async XLA Ops:
  129.4 15.8 %collective-permute-start = (f32[8,4096]{1,0:T(8,128)}, f32[8,4096]{1,0:T(8,128)}, u32[]{:S(2)}, u32[]{:S(2)}) collective-permute-start(f32[8,4096]{1,0:T(8,128)} %constant_dynamic-update-slice_fusion), channel_id=1, source_target_pairs={{0,4},{4,0},{1,5},{5,1},{2,6},{6,2},{3,7},{7,3}} | collective-permute-start | bytes 393224 | tf_op jit(solution)/shard_map/ppermute | solution.py:273
  219.1 246.1 %collective-permute-start.1 = (f32[1544,1024]{1,0:T(8,128)}, f32[1544,1024]{1,0:T(8,128)}, u32[]{:S(2)}, u32[]{:S(2)}) collective-permute-start(f32[1544,1024]{1,0:T(8,128)} %get-tuple-element.25), channel_id=1, source_target_pairs={{0,1},{1,0},{2,3},{3,2},{4,5},{5,4},{6,7},{7,6}} | collective-permute-start | bytes 18972680 | tf_op jit(solution)/shard_map/ppermute | solution.py:273
  219.2 20.8 %collective-permute-start.9 = (f32[1536,128]{1,0:T(8,128)}, f32[1536,128]{1,0:T(8,128)}, u32[]{:S(2)}, u32[]{:S(2)}) collective-permute-start(f32[1536,128]{1,0:T(8,128)} %cast.6), channel_id=1, source_target_pairs={{0,4},{4,0},{1,5},{5,1},{2,6},{6,2},{3,7},{7,3}} | collective-permute-start | bytes 2359304 | tf_op jit(solution)/shard_map/ppermute | solution.py:273
  222.1 74.0 %collective-permute-start.17 = (f32[5120,128]{1,0:T(8,128)}, f32[5120,128]{1,0:T(8,128)}, u32[]{:S(2)}, u32[]{:S(2)}) collective-permute-start(f32[5120,128]{1,0:T(8,128)} %cast.11), channel_id=1, source_target_pairs={{0,4},{4,0},{1,5},{5,1},{2,6},{6,2},{3,7},{7,3}} | collective-permute-start | bytes 7864328 | tf_op jit(solution)/shard_map/ppermute | solution.py:273
  227.2 125.0 %collective-permute-start.13 = (f32[5120,128]{1,0:T(8,128)}, f32[5120,128]{1,0:T(8,128)S(1)}, u32[]{:S(2)}, u32[]{:S(2)}) collective-permute-start(f32[5120,128]{1,0:T(8,128)} %cast.10), channel_id=1, source_target_pairs={{0,4},{4,0},{1,5},{5,1},{2,6},{6,2},{3,7},{7,3}} | collective-permute-start | bytes 7864328 | tf_op jit(solution)/shard_map/ppermute | solution.py:273
  239.9 18.8 %collective-permute-start.10 = (f32[1536,128]{1,0:T(8,128)}, f32[1536,128]{1,0:T(8,128)S(1)}, u32[]{:S(2)}, u32[]{:S(2)}) collective-permute-start(f32[1536,128]{1,0:T(8,128)} %collective-permute-done.9.rest_2_), channel_id=1, source_target_pairs={{0,2},{1,3},{2,0},{3,1},{4,6},{5,7},{6,4},{7,5}} | collective-permute-start | bytes 2359304 | tf_op jit(solution)/shard_map/ppermute | solution.py:273
  241.4 17.8 %collective-permute-start.11 = (f32[1536,128]{1,0:T(8,128)}, f32[1536,128]{1,0:T(8,128)S(1)}, u32[]{:S(2)}, u32[]{:S(2)}) collective-permute-start(f32[1536,128]{1,0:T(8,128)} %collective-permute-done.9.rest_2_), channel_id=1, source_target_pairs={{0,1},{1,0},{2,3},{3,2},{4,5},{5,4},{6,7},{7,6}} | collective-permute-start | bytes 2359304 | tf_op jit(solution)/shard_map/ppermute | solution.py:273
  258.7 206.5 %copy-start.8 = (f32[1536,128]{1,0:T(8,128)}, f32[1536,128]{1,0:T(8,128)S(1)}, u32[]{:S(2)}) copy-start(f32[1536,128]{1,0:T(8,128)S(1)} %collective-permute-done.10.rest_3_) | copy-start | bytes 2359300
  258.7 149.7 %collective-permute-start.3 = (f32[5120,128]{1,0:T(8,128)}, f32[5120,128]{1,0:T(8,128)}, u32[]{:S(2)}, u32[]{:S(2)}) collective-permute-start(f32[5120,128]{1,0:T(8,128)} %cast.8), channel_id=1, source_target_pairs={{0,4},{4,0},{1,5},{5,1},{2,6},{6,2},{3,7},{7,3}} | collective-permute-start | bytes 7864328 | tf_op jit(solution)/shard_map/ppermute | solution.py:273
  259.2 206.0 %copy-start.9 = (f32[1536,128]{1,0:T(8,128)}, f32[1536,128]{1,0:T(8,128)S(1)}, u32[]{:S(2)}) copy-start(f32[1536,128]{1,0:T(8,128)S(1)} %collective-permute-done.11.rest_4_) | copy-start | bytes 2359300
  259.2 2.3 collective-permute-start.12
  261.5 203.7 %copy-start.10 = (f32[1536,128]{1,0:T(8,128)}, f32[1536,128]{1,0:T(8,128)S(1)}, u32[]{:S(2)}) copy-start(f32[1536,128]{1,0:T(8,128)S(1)} %collective-permute-done.12.rest_5_) | copy-start | bytes 2359300
  261.5 203.1 %collective-permute-start.5 = (f32[5120,128]{1,0:T(8,128)}, f32[5120,128]{1,0:T(8,128)}, u32[]{:S(2)}, u32[]{:S(2)}) collective-permute-start(f32[5120,128]{1,0:T(8,128)} %cast.9), channel_id=1, source_target_pairs={{0,4},{4,0},{1,5},{5,1},{2,6},{6,2},{3,7},{7,3}} | collective-permute-start | bytes 7864328 | tf_op jit(solution)/shard_map/ppermute | solution.py:273
  296.1 168.5 %collective-permute-start.18 = (f32[5120,128]{1,0:T(8,128)}, f32[5120,128]{1,0:T(8,128)S(1)}, u32[]{:S(2)}, u32[]{:S(2)}) collective-permute-start(f32[5120,128]{1,0:T(8,128)} %collective-permute-done.17.rest_4_), channel_id=1, source_target_pairs={{0,2},{1,3},{2,0},{3,1},{4,6},{5,7},{6,4},{7,5}} | collective-permute-start | bytes 7864328 | tf_op jit(solution)/shard_map/ppermute | solution.py:273
  352.2 119.8 %copy-start.1 = (f32[5120,128]{1,0:T(8,128)}, f32[5120,128]{1,0:T(8,128)S(1)}, u32[]{:S(2)}) copy-start(f32[5120,128]{1,0:T(8,128)S(1)} %collective-permute-done.13.rest_0_) | copy-start | bytes 7864324
  352.2 113.0 %collective-permute-start.14 = (f32[5120,128]{1,0:T(8,128)S(1)}, f32[5120,128]{1,0:T(8,128)S(1)}, u32[]{:S(2)}, u32[]{:S(2)}) collective-permute-start(f32[5120,128]{1,0:T(8,128)S(1)} %collective-permute-done.13.rest_0_), channel_id=1, source_target_pairs={{0,2},{1,3},{2,0},{3,1},{4,6},{5,7},{6,4},{7,5}} | collective-permute-start | bytes 7864328 | tf_op jit(solution)/shard_map/ppermute | solution.py:273
  408.4 134.3 %collective-permute-start.7 = (f32[3584,256]{1,0:T(8,128)}, f32[3584,256]{1,0:T(8,128)}, u32[]{:S(2)}, u32[]{:S(2)}) collective-permute-start(f32[3584,256]{1,0:T(8,128)} %cast.7), channel_id=1, source_target_pairs={{0,4},{4,0},{1,5},{5,1},{2,6},{6,2},{3,7},{7,3}} | collective-permute-start | bytes 11010056 | tf_op jit(solution)/shard_map/ppermute | solution.py:273
  464.6 78.2 %collective-permute-start.19 = (f32[5120,128]{1,0:T(8,128)}, f32[5120,128]{1,0:T(8,128)S(1)}, u32[]{:S(2)}, u32[]{:S(2)}) collective-permute-start(f32[5120,128]{1,0:T(8,128)} %collective-permute-done.17.rest_4_), channel_id=1, source_target_pairs={{0,1},{1,0},{2,3},{3,2},{4,5},{5,4},{6,7},{7,6}} | collective-permute-start | bytes 7864328 | tf_op jit(solution)/shard_map/ppermute | solution.py:273
  464.6 7.4 copy-start.2
  464.6 78.7 %collective-permute-start.15 = (f32[5120,128]{1,0:T(8,128)S(1)}, f32[5120,128]{1,0:T(8,128)S(1)}, u32[]{:S(2)}, u32[]{:S(2)}) collective-permute-start(f32[5120,128]{1,0:T(8,128)S(1)} %collective-permute-done.13.rest_0_), channel_id=1, source_target_pairs={{0,1},{1,0},{2,3},{3,2},{4,5},{5,4},{6,7},{7,6}} | collective-permute-start | bytes 7864328 | tf_op jit(solution)/shard_map/ppermute | solution.py:273
  465.1 6.9 copy-start.3
  465.1 78.2 %collective-permute-start.20 = (f32[5120,128]{1,0:T(8,128)S(1)}, f32[5120,128]{1,0:T(8,128)S(1)}, u32[]{:S(2)}, u32[]{:S(2)}) collective-permute-start(f32[5120,128]{1,0:T(8,128)S(1)} %collective-permute-done.18.rest_5_), channel_id=1, source_target_pairs={{0,1},{1,0},{2,3},{3,2},{4,5},{5,4},{6,7},{7,6}} | collective-permute-start | bytes 7864328 | tf_op jit(solution)/shard_map/ppermute | solution.py:273
  465.2 79.6 %collective-permute-start.16 = (f32[5120,128]{1,0:T(8,128)S(1)}, f32[5120,128]{1,0:T(8,128)S(1)}, u32[]{:S(2)}, u32[]{:S(2)}) collective-permute-start(f32[5120,128]{1,0:T(8,128)S(1)} %collective-permute-done.14.rest_1_), channel_id=1, source_target_pairs={{0,1},{1,0},{2,3},{3,2},{4,5},{5,4},{6,7},{7,6}} | collective-permute-start | bytes 7864328 | tf_op jit(solution)/shard_map/ppermute | solution.py:273
  465.7 6.3 copy-start
  542.8 78.6 %collective-permute-start.4 = (f32[5120,128]{1,0:T(8,128)}, f32[5120,128]{1,0:T(8,128)}, u32[]{:S(2)}, u32[]{:S(2)}) collective-permute-start(f32[5120,128]{1,0:T(8,128)} %collective-permute-done.3.rest_0_), channel_id=1, source_target_pairs={{0,1},{1,0},{2,3},{3,2},{4,5},{5,4},{6,7},{7,6}} | collective-permute-start | bytes 7864328 | tf_op jit(solution)/shard_map/ppermute | solution.py:273
  542.8 2.1 copy-start.4
  542.8 182.1 %collective-permute-start.6 = (f32[5120,128]{1,0:T(8,128)}, f32[5120,128]{1,0:T(8,128)}, u32[]{:S(2)}, u32[]{:S(2)}) collective-permute-start(f32[5120,128]{1,0:T(8,128)} %collective-permute-done.5.rest_2_), channel_id=1, source_target_pairs={{0,1},{1,0},{2,3},{3,2},{4,5},{5,4},{6,7},{7,6}} | collective-permute-start | bytes 7864328 | tf_op jit(solution)/shard_map/ppermute | solution.py:273
  543.3 2.4 copy-start.5
  543.3 78.6 %collective-permute-start.8 = (f32[3584,256]{1,0:T(8,128)}, f32[3584,256]{1,0:T(8,128)}, u32[]{:S(2)}, u32[]{:S(2)}) collective-permute-start(f32[3584,256]{1,0:T(8,128)} %collective-permute-done.7.rest_0_), channel_id=1, source_target_pairs={{0,1},{1,0},{2,3},{3,2},{4,5},{5,4},{6,7},{7,6}} | collective-permute-start | bytes 11010056 | tf_op jit(solution)/shard_map/ppermute | solution.py:273
  543.3 2.7 copy-start.6
  543.4 78.6 %collective-permute-start.24 = (f32[768,1024]{1,0:T(8,128)}, f32[768,1024]{1,0:T(8,128)}, u32[]{:S(2)}, u32[]{:S(2)}) collective-permute-start(f32[768,1024]{1,0:T(8,128)} %slice_add_fusion.1.a_ref), channel_id=1, source_target_pairs={{0,2},{1,3},{2,0},{3,1},{4,6},{5,7},{6,4},{7,5}} | collective-permute-start | bytes 9437192 | tf_op jit(solution)/shard_map/ppermute | solution.py:273
  544.8 1.9 copy-start.7
  544.8 137.4 %collective-permute-start.2 = (f32[776,1024]{1,0:T(8,128)}, f32[776,1024]{1,0:T(8,128)}, u32[]{:S(2)}, u32[]{:S(2)}) collective-permute-start(f32[776,1024]{1,0:T(8,128)} %slice_add_fusion.a_ref), channel_id=1, source_target_pairs={{0,2},{1,3},{2,0},{3,1},{4,6},{5,7},{6,4},{7,5}} | collective-permute-start | bytes 9535496 | tf_op jit(solution)/shard_map/ppermute | solution.py:273
  621.3 152.7 %collective-permute-start.23 = (f32[768,1024]{1,0:T(8,128)}, f32[768,1024]{1,0:T(8,128)}, u32[]{:S(2)}, u32[]{:S(2)}) collective-permute-start(f32[768,1024]{1,0:T(8,128)} %slice_add_fusion.1.a_ref), channel_id=1, source_target_pairs={{0,1},{1,0},{2,3},{3,2},{4,5},{5,4},{6,7},{7,6}} | collective-permute-start | bytes 9437192 | tf_op jit(solution)/shard_map/ppermute | solution.py:273
  621.9 160.5 %collective-permute-start.21 = (f32[776,1024]{1,0:T(8,128)}, f32[776,1024]{1,0:T(8,128)}, u32[]{:S(2)}, u32[]{:S(2)}) collective-permute-start(f32[776,1024]{1,0:T(8,128)} %slice_add_fusion.a_ref), channel_id=1, source_target_pairs={{0,1},{1,0},{2,3},{3,2},{4,5},{5,4},{6,7},{7,6}} | collective-permute-start | bytes 9535496 | tf_op jit(solution)/shard_map/ppermute | solution.py:273
  621.9 152.1 %collective-permute-start.25 = (f32[768,1024]{1,0:T(8,128)}, f32[768,1024]{1,0:T(8,128)}, u32[]{:S(2)}, u32[]{:S(2)}) collective-permute-start(f32[768,1024]{1,0:T(8,128)} %collective-permute-done.24.b_ref), channel_id=1, source_target_pairs={{0,1},{1,0},{2,3},{3,2},{4,5},{5,4},{6,7},{7,6}} | collective-permute-start | bytes 9437192 | tf_op jit(solution)/shard_map/ppermute | solution.py:273
  682.3 100.1 %collective-permute-start.22 = (f32[776,1024]{1,0:T(8,128)}, f32[776,1024]{1,0:T(8,128)}, u32[]{:S(2)}, u32[]{:S(2)}) collective-permute-start(f32[776,1024]{1,0:T(8,128)} %collective-permute-done.2.b_ref), channel_id=1, source_target_pairs={{0,1},{1,0},{2,3},{3,2},{4,5},{5,4},{6,7},{7,6}} | collective-permute-start | bytes 9535496 | tf_op jit(solution)/shard_map/ppermute | solution.py:273
